TPU v7x, 8 devices: a whole 2x2x1 slice. The times are simulated.
8 devices in a mesh: data: 8 (over z, y, x, core).
Axes of the slice: x: 2, y: 2, z: 1, core: 2. Of those that a mesh axis runs over, the one named last changes fastest.
Arguments:
- gradient: float32 [3, 1769472], P(None, 'data')
- master: float32 [3, 1769472], P(None, 'data')
- moment_one: float32 [3, 1769472], P(None, 'data')
- moment_two: float32 [3, 1769472], P(None, 'data')
- tokens: bfloat16 [4096, 768], P('data')
- targets: bfloat16 [4096, 768], P('data')
Outputs:
- output 1: float32 [4096], P('data')
- output 2: bfloat16 [3, 1769472], replicated
- output 3: float32 [3, 1769472], P(None, 'data')
- output 4: float32 [3, 1769472], P(None, 'data')
- output 5: float32 [3, 1769472], P(None, 'data')
All inputs are finite; a program needn't handle non-finite values.
Results may differ from a plain program's by a relative error of at most 0.00174468.
Values are sent between devices in bfloat16 or wider.
A program may use at most 1 GiB of HBM per device.

v0:
```python
import jax
import jax.numpy as jnp
from jax import lax
from jax.sharding import PartitionSpec as P

LEARN_RATE = 0.01
BETA_ONE = 0.9
BETA_TWO = 0.95
ADAM_EPS = 1e-8
WEIGHT_DECAY = 0.1
ADAM_STEP = 10
CLIP_NORM = 1.0
NORM_EPS = 1e-6


def mlp_block(hidden, w_in, w_out):
    hidden_f32 = hidden.astype(jnp.float32)
    normed = (hidden_f32 * lax.rsqrt(jnp.mean(hidden_f32 * hidden_f32, axis=-1, keepdims=True) + NORM_EPS)).astype(jnp.bfloat16)
    inner = jnp.dot(normed, w_in, preferred_element_type=jnp.float32).astype(jnp.bfloat16)
    active = jax.nn.gelu(inner.astype(jnp.float32), approximate=True).astype(jnp.bfloat16)
    return (hidden_f32 + jnp.dot(active, w_out, preferred_element_type=jnp.float32)).astype(jnp.bfloat16)


def adam_update(grad_shard, master_shard, one_shard, two_shard, clip_scale):
    clipped = grad_shard * clip_scale
    new_one = BETA_ONE * one_shard + (1.0 - BETA_ONE) * clipped
    new_two = BETA_TWO * two_shard + (1.0 - BETA_TWO) * clipped * clipped
    step_size = (new_one / (1.0 - BETA_ONE ** ADAM_STEP)) / (jnp.sqrt(new_two / (1.0 - BETA_TWO ** ADAM_STEP)) + ADAM_EPS)
    new_master = master_shard - LEARN_RATE * (step_size + WEIGHT_DECAY * master_shard)
    return new_master, new_one, new_two


def solution(mesh):
    group_size = mesh.shape["data"]
    state_spec = P(None, "data")
    row_spec = P("data", None)

    def local_step(grad_shard, master_shard, one_shard, two_shard, tok_rows, tgt_rows):
        model_dim = tok_rows.shape[1]
        layers = master_shard.shape[0]
        half_size = master_shard.shape[1] * group_size // 2
        hidden_dim = half_size // model_dim
        sq_sum = lax.psum(jnp.sum(grad_shard * grad_shard), "data")
        clip_scale = jnp.minimum(1.0, CLIP_NORM / jnp.sqrt(sq_sum))
        new_master, new_one, new_two = adam_update(grad_shard, master_shard, one_shard, two_shard, clip_scale)
        new_bf16 = new_master.astype(jnp.bfloat16)
        gathered = [lax.all_gather(new_bf16[layer_idx], "data", tiled=True) for layer_idx in range(layers)]
        hidden = tok_rows
        for full_layer in gathered:
            w_in = full_layer[:half_size].reshape(model_dim, hidden_dim)
            w_out = full_layer[half_size:].reshape(hidden_dim, model_dim)
            hidden = mlp_block(hidden, w_in, w_out)
        error_val = hidden.astype(jnp.float32) - tgt_rows.astype(jnp.float32)
        row_loss = jnp.mean(error_val * error_val, axis=-1)
        return row_loss, jnp.stack(gathered), new_master, new_one, new_two

    return jax.shard_map(local_step, mesh=mesh, in_specs=(state_spec, state_spec, state_spec, state_spec, row_spec, row_spec), out_specs=(P("data"), P(), state_spec, state_spec, state_spec), check_vma=False)
```

profile of v0, /device:TPU:0, one launch (start us, length us, event | category | flops | bytes accessed | tf_op | source)
XLA Modules:
  0.0 281.3 jit_solution(8326925497367815126)
XLA Ops:
  7.2 0.0 copy-start
  7.2 0.0 all-gather.7.cloned.1.call-start
  7.2 4.3 %multiply_reduce_fusion = f32[]{:T(128)} fusion(f32[3,221184]{1,0:T(4,128)} %param.6), kind=kLoop, calls=%fused_computation.23 | loop fusion | flops 1327103 | bytes 2654212 | tf_op jit(solution)/shard_map/reduce_sum | solution.py:43
  11.5 25.3 %psum.7 = f32[]{:T(128)} all-reduce(f32[]{:T(128)} %multiply_reduce_fusion), channel_id=1, replica_groups=mesh['data'=8] {'data'}, use_global_device_ids=true, to_apply=%region_2.0 | all-reduce | flops 1 | bytes 8 | tf_op jit(solution)/shard_map/psum | solution.py:43
  37.5 0.0 copy-done
  37.5 11.1 %fusion.55 = (bf16[3,221184]{1,0:T(4,128)(2,1)S(1)}, f32[3,221184]{1,0:T(4,128)}, f32[3,221184]{1,0:T(4,128)}, f32[3,221184]{1,0:T(4,128)}) fusion(f32[3,221184]{1,0:T(4,128)} %param.7, f32[3,221184]{1,0:T(4,128)S(1)} %copy-done, f32[]{:T(128)S(6)} %min.3, f32[3,221184]{1,0:T(4,128)} %param.8, f32[3,221184]{1,0:T(4,128)} %param.9), kind=kLoop, calls=%fused_computation.83 | loop fusion | flops 11280384 | bytes 19906564 | tf_op jit(solution)/shard_map/convert_element_type | solution.py:46
  48.6 3.1 %fusion.57 = (bf16[1,221184]{1,0:T(2,128)(2,1)}, bf16[1,221184]{1,0:T(2,128)(2,1)}, bf16[1,221184]{1,0:T(2,128)(2,1)}) fusion(bf16[3,221184]{1,0:T(4,128)(2,1)S(1)} %get-tuple-element.11), kind=kLoop, calls=%fused_computation.84 | loop fusion | bytes 2654208 | tf_op jit(solution)/shard_map/slice | solution.py:47
  51.7 0.0 copy-start.4
  51.7 0.0 all-gather.7.cloned.1.call-update
  51.7 0.0 all-gather.9.cloned.1.call-start
  51.7 0.7 all-gather.9.cloned.1.call-update
  52.4 0.2 all-gather.11.cloned.1.call-start
  52.6 0.5 all-gather.11.cloned.1.call-update
  53.2 0.0 copy-done.4
  53.2 0.2 fusion.19
  53.4 42.3 %all-gather.7.cloned.1.call-done = bf16[1,1769472]{1,0:T(2,128)(2,1)} async-done(((bf16[1,221184]{1,0:T(2,128)(2,1)}), bf16[1,1769472]{1,0:T(2,128)(2,1)}) %all-gather.7.cloned.1.call-update) | async-done | bytes 3538960 | tf_op jit(solution)/shard_map/all_gather | solution.py:47
  95.7 39.1 %slice_reduce_fusion.5 = (bf16[884736]{0:T(1024)(128)(2,1)S(1)}, bf16[884736]{0:T(1024)(128)(2,1)S(1)}) fusion(bf16[1,1769472]{1,0:T(2,128)(2,1)} %all-gather.7.cloned.1.call-done), kind=kLoop, calls=%fused_computation.20 | loop fusion | bytes 7077888 | tf_op jit(solution)/shard_map/slice | solution.py:50
  134.8 3.1 %slice.89 = bf16[768,1152]{1,0:T(8,128)(2,1)} reshape(bf16[884736]{0:T(1024)(128)(2,1)S(1)} %get-tuple-element.9) | data formatting | bytes 3538944 | tf_op jit(solution)/shard_map/slice | solution.py:50
  137.9 2.7 slice.91
  140.6 0.4 all-gather.9.cloned.1.call-done
  140.9 39.3 %slice_reduce_fusion.3 = (bf16[884736]{0:T(1024)(128)(2,1)S(1)}, bf16[884736]{0:T(1024)(128)(2,1)S(1)}) fusion(bf16[1,1769472]{1,0:T(2,128)(2,1)} %all-gather.9.cloned.1.call-done), kind=kLoop, calls=%fused_computation.18 | loop fusion | bytes 7077888 | tf_op jit(solution)/shard_map/slice | solution.py:50
  180.2 3.0 %slice.94 = bf16[768,1152]{1,0:T(8,128)(2,1)} reshape(bf16[884736]{0:T(1024)(128)(2,1)S(1)} %get-tuple-element.7) | data formatting | bytes 3538944 | tf_op jit(solution)/shard_map/slice | solution.py:50
  183.3 0.0 copy-start.1
  183.3 2.7 slice.96
  185.9 0.0 copy-done.1
  185.9 0.0 copy-start.2
  185.9 5.4 %fusion.22 = (f32[512]{0:T(512)S(1)}, bf16[512,768]{1,0:T(8,128)(2,1)}) fusion(bf16[1152,768]{1,0:T(8,128)(2,1)} %slice.91, bf16[768,1152]{1,0:T(8,128)(2,1)S(1)} %copy-done.1, bf16[512,768]{1,0:T(8,128)(2,1)} %param.10, f32[512]{0:T(512)S(1)} %add_rsqrt_fusion.2), kind=kOutput, calls=%fused_computation.57 | convolution fusion | flops 1821965824 | bytes 5115904 | tf_op jit(solution)/shard_map/dot_general | solution.py:21
  191.4 0.0 copy-done.2
  191.4 5.3 %fusion.25 = (f32[512]{0:T(512)S(1)}, bf16[512,768]{1,0:T(8,128)(2,1)}) fusion(bf16[1152,768]{1,0:T(8,128)(2,1)} %slice.96, bf16[768,1152]{1,0:T(8,128)(2,1)S(1)} %copy-done.2, bf16[512,768]{1,0:T(8,128)(2,1)} %get-tuple-element.19, f32[512]{0:T(512)S(1)} %add_rsqrt_fusion.1), kind=kOutput, calls=%fused_computation.60 | convolution fusion | flops 1821965824 | bytes 5115904 | tf_op jit(solution)/shard_map/dot_general | solution.py:21
  196.7 0.0 all-gather.11.cloned.1.call-done
  196.7 39.4 %slice_reduce_fusion.1 = (bf16[884736]{0:T(1024)(128)(2,1)S(1)}, bf16[884736]{0:T(1024)(128)(2,1)S(1)}) fusion(bf16[1,1769472]{1,0:T(2,128)(2,1)} %all-gather.11.cloned.1.call-done), kind=kLoop, calls=%fused_computation.16 | loop fusion | bytes 7077888 | tf_op jit(solution)/shard_map/slice | solution.py:50
  236.1 2.7 slice.101
  238.8 0.0 copy-start.3
  238.8 3.0 %slice.99 = bf16[768,1152]{1,0:T(8,128)(2,1)} reshape(bf16[884736]{0:T(1024)(128)(2,1)S(1)} %get-tuple-element.5) | data formatting | bytes 3538944 | tf_op jit(solution)/shard_map/slice | solution.py:50
  241.8 0.0 copy-done.3
  241.8 4.7 %multiply_reduce_fusion.1 = f32[512]{0:T(512)S(1)} fusion(bf16[512,768]{1,0:T(8,128)(2,1)} %param.11, bf16[1152,768]{1,0:T(8,128)(2,1)S(1)} %copy-done.3, bf16[512,768]{1,0:T(8,128)(2,1)} %get-tuple-element.21, bf16[768,1152]{1,0:T(8,128)(2,1)} %slice.99, f32[512]{0:T(512)S(1)} %add_rsqrt_fusion), kind=kOutput, calls=%fused_computation.63 | convolution fusion | flops 1822752256 | bytes 5115904 | tf_op jit(solution)/shard_map/dot_general | solution.py:21
  246.5 0.6 broadcast_multiply_fusion
  247.1 27.2 %pad_maximum_fusion = bf16[3,1769472]{1,0:T(4,128)(2,1)} fusion(bf16[1,1769472]{1,0:T(2,128)(2,1)} %all-gather.11.cloned.1.call-done, bf16[1,1769472]{1,0:T(2,128)(2,1)} %all-gather.9.cloned.1.call-done, bf16[1,1769472]{1,0:T(2,128)(2,1)} %all-gather.7.cloned.1.call-done), kind=kLoop, calls=%fused_computation | loop fusion | flops 31850496 | bytes 21233664 | tf_op jit(solution)/shard_map/stack | solution.py:55
  (3 shorter events, 0.0 us)
Async XLA Ops:
  7.2 30.3 %copy-start = (f32[3,221184]{1,0:T(4,128)S(1)}, f32[3,221184]{1,0:T(4,128)}, u32[]{:S(2)}) copy-start(f32[3,221184]{1,0:T(4,128)} %param.6) | copy-start | bytes 7962628
  7.2 88.5 %all-gather.7.cloned.1.call-start = ((), (), s32[]{:S(2)}) async-start(), calls=%async_computation | async-start | bytes 7962624 | tf_op jit(solution)/shard_map/all_gather | solution.py:47
  51.7 1.5 copy-start.4
  51.7 89.2 %all-gather.9.cloned.1.call-start = ((), (), s32[]{:S(2)}) async-start(), calls=%async_computation.1 | async-start | bytes 7962624 | tf_op jit(solution)/shard_map/all_gather | solution.py:47
  52.4 144.3 %all-gather.11.cloned.1.call-start = ((), (), s32[]{:S(2)}) async-start(), calls=%async_computation.2 | async-start | bytes 7962624 | tf_op jit(solution)/shard_map/all_gather | solution.py:47
  183.3 2.7 copy-start.1
  185.9 5.4 %copy-start.2 = (bf16[768,1152]{1,0:T(8,128)(2,1)S(1)}, bf16[768,1152]{1,0:T(8,128)(2,1)}, u32[]{:S(2)}) copy-start(bf16[768,1152]{1,0:T(8,128)(2,1)} %slice.94) | copy-start | bytes 5308420
  238.8 3.0 %copy-start.3 = (bf16[1152,768]{1,0:T(8,128)(2,1)S(1)}, bf16[1152,768]{1,0:T(8,128)(2,1)}, u32[]{:S(2)}) copy-start(bf16[1152,768]{1,0:T(8,128)(2,1)} %slice.101) | copy-start | bytes 5308420
Sparse Core Ops, SparseCore 0:
  51.8 43.8 all-gather.6
  98.1 42.8 all-gather.8
  142.7 42.8 all-gather.10
where the time goes:
time: 286 us; the launch traced here: 281 us
  local copies, waits for them, and re-layouts  138 us (48%)
  waiting for transfers between devices  43.8 us (15%)
  other arithmetic  43.4 us (15%)
  blocking collectives  25.3 us (9%)
  matrix products  15.5 us (5%)
  between operations  14.9 us (5%)
    slice x6, local copies, waits for them, and re-layouts, local_step(): w_in = full_layer[:half_size].reshape(model_dim, hidden_dim)  127 us
    all_gather x3, waiting for transfers between devices, local_step(): lax.all_gather(new_bf16[layer_idx], 'data', tiled=True)  42.6 us
    another operation x1, other arithmetic, local_step(): return (row_loss, jnp.stack(gathered), new_master, new_one, new_two)  27.2 us
    psum x1, blocking collectives, local_step(): sq_sum = lax.psum(jnp.sum(grad_shard * grad_shard), 'data')  25.3 us
    dot_general x3, matrix products, mlp_block(): jnp.dot(active, w_out, preferred_element_type=jnp.float32)  15.5 us
    convert_element_type x1, other arithmetic, local_step(): new_bf16 = new_master.astype(jnp.bfloat16)  11.1 us
    slice x3, local copies, waits for them, and re-layouts, local_step(): w_out = full_layer[half_size:].reshape(hidden_dim, model_dim)  8 us
  transfers between devices with their start and end apart: 3, of which 2 were waited for; matrix products, arithmetic and copies ran while one was open for 36% of the time, Pallas kernels for 0%

commit v1 on v0

v1 whole, which is shorter than its diff:
```python
import functools

import jax
import jax.numpy as jnp
from jax import lax
from jax.experimental import pallas as pl
from jax.experimental.pallas import tpu as pltpu
from jax.sharding import PartitionSpec as P

LEARN_RATE = 0.01
BETA_ONE = 0.9
BETA_TWO = 0.95
ADAM_EPS = 1e-8
WEIGHT_DECAY = 0.1
ADAM_STEP = 10
CLIP_NORM = 1.0
NORM_EPS = 1e-6

MESH = pl.DeviceIdType.MESH
LANES = 128
GROUP = 8
F32 = jnp.float32
BF16 = jnp.bfloat16


def gather_kernel(dims, grad_hbm, master_hbm, one_hbm, two_hbm, tok_hbm, tgt_hbm,
                  packed_ref, master_out, one_out, two_out, loss_ref,
                  w_in, w_out, grad_v, master_v, one_v, two_v, tok_v, tgt_v,
                  part_ref, wide_ref, normed_ref, active_ref, hidden_ref,
                  load_sem, part_send, part_recv, send_sem, recv_sem):
    layers, model_dim, hidden_dim, rows, chunks = dims
    in_rows = chunks * LANES // hidden_dim
    out_rows = chunks * LANES // model_dim
    half_chunks = chunks // 2

    me = lax.axis_index("data")
    core = lax.rem(me, 2)
    x_pos = lax.rem(me // 2, 2)
    y_pos = me // 4
    partner = me + 1 - 2 * core
    x_peer = me + 2 - 4 * x_pos
    y_peer = me + 4 - 8 * y_pos
    diag = x_peer + 4 - 8 * y_pos

    state = ((grad_hbm, grad_v), (master_hbm, master_v), (one_hbm, one_v), (two_hbm, two_v))

    def load(which, layer):
        src, dst = state[which]
        return pltpu.make_async_copy(src.at[:, layer, :], dst.at[layer], load_sem.at[which, layer])

    for which in range(4):
        for layer in range(layers):
            load(which, layer).start()
    tok_load = pltpu.make_async_copy(tok_hbm, tok_v, load_sem.at[4, 0])
    tgt_load = pltpu.make_async_copy(tgt_hbm, tgt_v, load_sem.at[4, 1])
    tok_load.start()
    tgt_load.start()

    barrier = pltpu.get_barrier_semaphore()
    for step in range(1, GROUP):
        pl.semaphore_signal(barrier, inc=1, device_id=(lax.rem(me + step, GROUP),), device_id_type=MESH)

    sums = tuple(jnp.zeros((8, LANES), F32) for _ in range(8))
    for layer in range(layers):
        load(0, layer).wait()

        def square(idx, carry):
            base = pl.multiple_of(idx * 64, 64)
            block = grad_v[layer, pl.ds(base, 64), :]
            return tuple(carry[k] + block[8 * k:8 * k + 8] * block[8 * k:8 * k + 8] for k in range(8))

        sums = lax.fori_loop(0, chunks // 64, square, sums)
    mine = ((sums[0] + sums[1]) + (sums[2] + sums[3])) + ((sums[4] + sums[5]) + (sums[6] + sums[7]))
    part_ref[me] = mine
    pl.semaphore_wait(barrier, GROUP - 1)

    def part_copy(step):
        return pltpu.make_async_remote_copy(
            src_ref=part_ref.at[me], dst_ref=part_ref.at[me],
            send_sem=part_send.at[step], recv_sem=part_recv.at[step],
            device_id=(lax.rem(me + step, GROUP),), device_id_type=MESH)

    def part_arrival(step):
        slot = lax.rem(me + GROUP - step, GROUP)
        return pltpu.make_async_remote_copy(
            src_ref=part_ref.at[slot], dst_ref=part_ref.at[slot],
            send_sem=part_send.at[step], recv_sem=part_recv.at[step],
            device_id=(me,), device_id_type=MESH)

    for step in range(1, GROUP):
        part_copy(step).start()
    for step in range(1, GROUP):
        part_arrival(step).wait_recv()
    total = part_ref[0]
    for slot in range(1, GROUP):
        total = total + part_ref[slot]
    total = jnp.sum(jnp.sum(total, axis=0, keepdims=True), axis=1, keepdims=True)
    clip = jnp.minimum(1.0, CLIP_NORM / jnp.sqrt(total))
    clip = jnp.broadcast_to(clip, (8, LANES))

    def piece(kind, layer, device, half):
        slot = lax.rem(device, 4)
        if kind == 0:
            return w_in.at[layer, pl.ds(pl.multiple_of(slot * in_rows + half * (in_rows // 2), 16), in_rows // 2), :]
        return w_out.at[layer, pl.ds(pl.multiple_of(slot * out_rows + half * (out_rows // 2), 16), out_rows // 2), :]

    def copy(kind, layer, device, half, index, target):
        ref = piece(kind, layer, device, half)
        return pltpu.make_async_remote_copy(
            src_ref=ref, dst_ref=ref, send_sem=send_sem.at[layer, index],
            recv_sem=recv_sem.at[layer, index], device_id=(target,), device_id_type=MESH)

    def by_kind(function):
        for y_value in range(2):
            @pl.when(y_pos == y_value)
            def _():
                function(y_value)

    one_scale = 1.0 / (1.0 - BETA_ONE ** ADAM_STEP)
    two_scale = 1.0 / (1.0 - BETA_TWO ** ADAM_STEP)

    def adam(layer, half):
        def update(idx, _):
            base = pl.multiple_of(half * half_chunks + idx * 48, 8)
            for k in range(6):
                at = pl.ds(pl.multiple_of(base + 8 * k, 8), 8)
                clipped = grad_v[layer, at, :] * clip
                new_one = BETA_ONE * one_v[layer, at, :] + (1.0 - BETA_ONE) * clipped
                new_two = BETA_TWO * two_v[layer, at, :] + (1.0 - BETA_TWO) * clipped * clipped
                step_size = (new_one * one_scale) / (jnp.sqrt(new_two * two_scale) + ADAM_EPS)
                old = master_v[layer, at, :]
                master_out[layer, at, :] = old - LEARN_RATE * (step_size + WEIGHT_DECAY * old)
                one_out[layer, at, :] = new_one
                two_out[layer, at, :] = new_two
            return 0

        lax.fori_loop(0, half_chunks // 48, update, 0)

    def round_rows(kind, layer, half):
        width = hidden_dim if kind == 0 else model_dim
        count = in_rows if kind == 0 else out_rows
        per_row = width // LANES
        dst = w_in if kind == 0 else w_out
        slot = lax.rem(me, 4)

        def body(idx, _):
            base = half * half_chunks + idx * (16 * per_row)
            row = pl.multiple_of(slot * count + half * (count // 2) + idx * 16, 16)
            for col in range(per_row):
                top = master_out[layer, pl.ds(base + col, 8, stride=per_row), :]
                low = master_out[layer, pl.ds(base + 8 * per_row + col, 8, stride=per_row), :]
                dst[layer, pl.ds(row, 16), col * LANES:(col + 1) * LANES] = jnp.concatenate([top, low], axis=0).astype(BF16)
            return 0

        lax.fori_loop(0, count // 32, body, 0)

    for layer in range(layers):
        for which in range(1, 4):
            load(which, layer).wait()
        for half in range(2):
            adam(layer, half)

            def send_own(kind):
                round_rows(kind, layer, half)
                copy(kind, layer, me, half, half, x_peer).start()
                copy(kind, layer, me, half, 2 + half, y_peer).start()
                copy(kind, layer, me, half, 6 + half, partner).start()

            by_kind(send_own)

    def pack(kind, device):
        width = hidden_dim if kind == 0 else model_dim
        count = in_rows if kind == 0 else out_rows
        per_row = width // LANES
        src = w_in if kind == 0 else w_out
        slot = lax.rem(device, 4)

        def spread(idx, _):
            row = pl.multiple_of(slot * count + idx * 16, 16)
            for layer in range(layers):
                for col in range(per_row):
                    tile = src[layer, pl.ds(row, 16), col * LANES:(col + 1) * LANES].astype(F32)
                    base = layer + 4 * (idx * (16 * per_row) + col)
                    wide_ref[pl.ds(base, 8, stride=4 * per_row), :] = tile[0:8]
                    wide_ref[pl.ds(base + 32 * per_row, 8, stride=4 * per_row), :] = tile[8:16]
            return 0

        lax.fori_loop(0, count // 16, spread, 0)

        def squeeze(idx, _):
            src_at = pl.multiple_of(idx * 128, 128)
            block = wide_ref[pl.ds(src_at, 128), :].astype(BF16).reshape(32, 4, LANES)
            packed_ref[pl.ds(device * chunks + idx * 32, 32), :, :] = block[:, :layers, :]
            return 0

        lax.fori_loop(0, 4 * chunks // 128, squeeze, 0)

    def partner_of(device):
        return device + 1 - 2 * core

    def mlp(layer):
        def block(idx, _):
            at = pl.ds(pl.multiple_of(idx * 256, 256), 256)
            hidden = hidden_ref[at, :].astype(F32)
            scale = lax.rsqrt(jnp.mean(hidden * hidden, axis=-1, keepdims=True) + NORM_EPS)
            normed_ref[...] = (hidden * scale).astype(BF16)
            for col in range(0, hidden_dim, 384):
                inner = jnp.dot(normed_ref[...], w_in[layer, :, col:col + 384], preferred_element_type=F32).astype(BF16)
                active_ref[:, col:col + 384] = jax.nn.gelu(inner.astype(F32), approximate=True).astype(BF16)
            for col in range(0, model_dim, 256):
                add = jnp.dot(active_ref[...], w_out[layer, :, col:col + 256], preferred_element_type=F32)
                hidden_ref[at, col:col + 256] = (hidden_ref[at, col:col + 256].astype(F32) + add).astype(BF16)
            return 0

        lax.fori_loop(0, rows // 256, block, 0)

    tok_load.wait()
    tgt_load.wait()
    hidden_ref[...] = tok_v[...]

    for layer in range(layers):
        def forward(kind):
            for half in range(2):
                copy(kind, layer, x_peer, half, half, me).wait_recv()
                if half == 0:
                    copy(kind, layer, x_peer, half, 4, y_peer).start()
                copy(kind, layer, x_peer, half, 8 + half, partner).start()
                copy(1 - kind, layer, y_peer, half, 2 + half, me).wait_recv()
                if half == 1:
                    copy(1 - kind, layer, y_peer, half, 5, x_peer).start()
                copy(1 - kind, layer, y_peer, half, 10 + half, partner).start()
            for half in range(2):
                copy(kind, layer, partner, half, 6 + half, me).wait_recv()

        by_kind(forward)

    def pack_near(kind):
        pack(kind, me)
        pack(kind, partner)
        pack(kind, x_peer)
        pack(1 - kind, y_peer)
        for layer in range(layers):
            for half in range(2):
                copy(kind, layer, partner_of(x_peer), half, 8 + half, me).wait_recv()
                copy(1 - kind, layer, partner_of(y_peer), half, 10 + half, me).wait_recv()
        pack(kind, partner_of(x_peer))
        pack(1 - kind, partner_of(y_peer))

    by_kind(pack_near)

    for layer in range(layers):
        def far(kind):
            for half in range(2):
                copy(1 - kind, layer, diag, half, 4 + half, me).wait_recv()
                copy(1 - kind, layer, diag, half, 12 + half, partner).start()
            for half in range(2):
                copy(1 - kind, layer, partner_of(diag), half, 12 + half, me).wait_recv()

        by_kind(far)
        mlp(layer)

    def pack_far(kind):
        pack(1 - kind, diag)
        pack(1 - kind, partner_of(diag))

    by_kind(pack_far)

    for idx in range(rows // LANES):
        at = slice(idx * LANES, (idx + 1) * LANES)
        error = hidden_ref[at, :].astype(F32) - tgt_v[at, :].astype(F32)
        error = error * error
        folded = error[:, 0:LANES]
        for col in range(LANES, model_dim, LANES):
            folded = folded + error[:, col:col + LANES]
        loss_ref[idx:idx + 1, :] = jnp.sum(folded.T, axis=0, keepdims=True) * (1.0 / model_dim)

    for step in range(1, GROUP):
        part_copy(step).wait_send()

    def drain(kind):
        for layer in range(layers):
            for half in range(2):
                copy(kind, layer, me, half, half, x_peer).wait_send()
                copy(kind, layer, me, half, 2 + half, y_peer).wait_send()
                copy(kind, layer, me, half, 6 + half, partner).wait_send()
                copy(kind, layer, x_peer, half, 8 + half, partner).wait_send()
                copy(1 - kind, layer, y_peer, half, 10 + half, partner).wait_send()
                copy(1 - kind, layer, diag, half, 12 + half, partner).wait_send()
            copy(kind, layer, x_peer, 0, 4, y_peer).wait_send()
            copy(1 - kind, layer, y_peer, 1, 5, x_peer).wait_send()

    by_kind(drain)


def write_kernel(layers, pieces, packed_ref, master_ref, one_ref, two_ref, loss_ref,
                 packed_hbm, master_hbm, one_hbm, two_hbm, loss_hbm, sem):
    copies = [pltpu.make_async_copy(loss_ref, loss_hbm, sem.at[0])]
    span = packed_ref.shape[0] // pieces
    for idx in range(pieces):
        at = pl.ds(idx * span, span)
        copies.append(pltpu.make_async_copy(packed_ref.at[at], packed_hbm.at[at], sem.at[1 + idx]))
    for which, (src, dst) in enumerate(((master_ref, master_hbm), (one_ref, one_hbm), (two_ref, two_hbm))):
        for layer in range(layers):
            copies.append(pltpu.make_async_copy(src.at[layer], dst.at[:, layer, :], sem.at[1 + pieces + which * layers + layer]))
    for item in copies:
        item.start()
    for item in copies:
        item.wait()


def solution(mesh):
    group_size = mesh.shape["data"]
    state_spec = P(None, "data")
    row_spec = P("data", None)

    def local_step(grad_shard, master_shard, one_shard, two_shard, tok_rows, tgt_rows):
        rows, model_dim = tok_rows.shape
        layers, cols = master_shard.shape
        half_size = cols * group_size // 2
        hidden_dim = half_size // model_dim
        chunks = cols // LANES
        dims = (layers, model_dim, hidden_dim, rows, chunks)
        tiled = [a.reshape(layers, chunks, LANES).transpose(1, 0, 2) for a in (grad_shard, master_shard, one_shard, two_shard)]
        state_v = pltpu.VMEM((layers, chunks, LANES), F32)
        hbm = pl.BlockSpec(memory_space=pltpu.HBM)
        vmem = pl.BlockSpec(memory_space=pltpu.VMEM)
        state_out = state_v
        packed, new_master, new_one, new_two, loss = pl.pallas_call(
            functools.partial(gather_kernel, dims),
            name="gather_step",
            out_shape=(pltpu.VMEM((chunks * group_size, layers, LANES), BF16), state_out, state_out, state_out,
                       jax.ShapeDtypeStruct((rows // LANES, LANES), F32)),
            in_specs=[hbm] * 6,
            out_specs=(vmem,) * 5,
            scratch_shapes=[
                pltpu.VMEM((layers, model_dim, hidden_dim), BF16),
                pltpu.VMEM((layers, hidden_dim, model_dim), BF16),
                state_v, state_v, state_v, state_v,
                pltpu.VMEM((rows, model_dim), BF16),
                pltpu.VMEM((rows, model_dim), BF16),
                pltpu.VMEM((group_size, 8, LANES), F32),
                pltpu.VMEM((4 * chunks, LANES), F32),
                pltpu.VMEM((256, model_dim), BF16),
                pltpu.VMEM((256, hidden_dim), BF16),
                pltpu.VMEM((rows, model_dim), BF16),
                pltpu.SemaphoreType.DMA((5, layers)),
                pltpu.SemaphoreType.DMA((group_size,)),
                pltpu.SemaphoreType.DMA((group_size,)),
                pltpu.SemaphoreType.DMA((layers, 14)),
                pltpu.SemaphoreType.DMA((layers, 14)),
            ],
            compiler_params=pltpu.CompilerParams(collective_id=0, has_side_effects=True, vmem_limit_bytes=28 << 20),
        )(*[pltpu.with_memory_space_constraint(a, pltpu.HBM) for a in (*tiled, tok_rows, tgt_rows)])
        state_tile = jax.ShapeDtypeStruct((chunks, layers, LANES), F32)
        pieces = 8
        weights, new_master, new_one, new_two, row_loss = pl.pallas_call(
            functools.partial(write_kernel, layers, pieces),
            name="write_out",
            out_shape=(jax.ShapeDtypeStruct((chunks * group_size, layers, LANES), BF16), state_tile, state_tile, state_tile,
                       jax.ShapeDtypeStruct((rows // LANES, LANES), F32)),
            in_specs=[vmem] * 5,
            out_specs=(hbm,) * 5,
            scratch_shapes=[pltpu.SemaphoreType.DMA((1 + pieces + 3 * layers,))],
            compiler_params=pltpu.CompilerParams(vmem_limit_bytes=2 << 20),
        )(packed, new_master, new_one, new_two, loss)

        def flat(a):
            return a.transpose(1, 0, 2).reshape(layers, a.shape[0] * LANES)

        return row_loss.reshape(rows), flat(weights), flat(new_master), flat(new_one), flat(new_two)

    return jax.shard_map(local_step, mesh=mesh, in_specs=(state_spec, state_spec, state_spec, state_spec, row_spec, row_spec), out_specs=(P("data"), P(), state_spec, state_spec, state_spec), check_vma=False)
```

time: 286 us -> 74 us (0.26); the launches traced: 281 us -> 73.3 us
  local copies, waits for them, and re-layouts: 138 us -> 0 us
  Pallas kernels: 0 us -> 72.6 us
  waiting for transfers between devices: 43.8 us -> 0 us
  other arithmetic: 43.4 us -> 0 us
  blocking collectives: 25.3 us -> 0 us
  matrix products: 15.5 us -> 0 us
  between operations: 14.9 us -> 0.64 us
    slice x10 -> x0, local copies, waits for them, and re-layouts: 138 us -> none  [the longest x6 127 us: local_step(): w_in = full_layer[:half_size].reshape(model_dim, hidden_dim)]
    pallas_call x0 -> x2, Pallas kernels: none -> 72.6 us  [the longest x1 65 us: local_step(): pl.pallas_call(functools.partial(gather_kernel, dims), name='gather_step'...]
    all_gather x3 -> x0, waiting for transfers between devices: 42.6 us -> none  [local_step(): lax.all_gather(new_bf16[layer_idx], 'data', tiled=True)]
    another operation x1 -> x0, other arithmetic: 27.2 us -> none  [local_step(): return (row_loss, jnp.stack(gathered), new_master, new_one, new_two)]
    psum x1 -> x0, blocking collectives: 25.3 us -> none  [local_step(): sq_sum = lax.psum(jnp.sum(grad_shard * grad_shard), 'data')]
    dot_general x3 -> x0, matrix products: 15.5 us -> none  [mlp_block(): jnp.dot(active, w_out, preferred_element_type=jnp.float32)]
    convert_element_type x1 -> x0, other arithmetic: 11.1 us -> none  [local_step(): new_bf16 = new_master.astype(jnp.bfloat16)]
    reduce_sum x2 -> x0, other arithmetic: 4.51 us -> none  [the longest x1 4.28 us: local_step(): sq_sum = lax.psum(jnp.sum(grad_shard * grad_shard), 'data')]
  transfers between devices with their start and end apart: 3 -> 0, of which waited for: 2 -> 0; matrix products, arithmetic and copies ran while one was open for 36% -> 0% of each run, Pallas kernels for 0% -> 0%
where the time goes in v1:
time: 74 us; the launch traced here: 73.3 us
  Pallas kernels  72.6 us (98%)
    pallas_call x1, Pallas kernels, local_step(): pl.pallas_call(functools.partial(gather_kernel, dims), name='gather_step'...  65 us
    pallas_call x1, Pallas kernels, local_step(): pl.pallas_call(functools.partial(write_kernel, layers, pieces), name='wri...  7.61 us

profile of v1, /device:TPU:0, one launch (start us, length us, event | category | flops | bytes accessed | tf_op | source)
XLA Modules:
  0.0 73.3 jit_solution(5173098383963428596)
XLA Ops:
  0.6 65.0 %gather_step.1 = (bf16[13824,3,128]{2,1,0:T(4,128)(2,1)S(1)}, f32[3,1728,128]{2,1,0:T(8,128)S(1)}, f32[3,1728,128]{2,1,0:T(8,128)S(1)}, f32[3,1728,128]{2,1,0:T(8,128)S(1)}, f32[4,128]{1,0:T(4,128)S(1)}) custom-call(f32[1728,3,128]{2,1,0:T(4,128)} %bitcast.25, f32[1728,3,128]{2,1,0:T(4,128)} %bitcast.26, f32[1728,3,128]{2,1,0:T(4,128)} %bitcast.27, ...), custom_call_target="tpu_custom_call" | custom-call | tf_op jit(solution)/shard_map/gather_step/pallas_call | solution.py:328
  65.6 7.6 %write_out.1 = (bf16[13824,3,128]{2,1,0:T(4,128)(2,1)}, f32[1728,3,128]{2,1,0:T(4,128)}, f32[1728,3,128]{2,1,0:T(4,128)}, f32[1728,3,128]{2,1,0:T(4,128)}, f32[4,128]{1,0:T(4,128)}) custom-call(bf16[13824,3,128]{2,1,0:T(4,128)(2,1)S(1)} %get-tuple-element.15.packed_ref, f32[3,1728,128]{2,1,0:T(8,128)S(1)} %get-tuple-element.16.master_ref, ...), custom_call_target="tpu_custom_call" | custom-call | tf_op jit(solution)/shard_map/write_out/pallas_call | solution.py:356

commit v2 on v1

--- a/solution.py
+++ b/solution.py
@@ -23,24 +23,67 @@
 BF16 = jnp.bfloat16
 
 
-def gather_kernel(dims, grad_hbm, master_hbm, one_hbm, two_hbm, tok_hbm, tgt_hbm,
-                  packed_ref, master_out, one_out, two_out, loss_ref,
-                  w_in, w_out, grad_v, master_v, one_v, two_v, tok_v, tgt_v,
-                  part_ref, wide_ref, normed_ref, active_ref, hidden_ref,
+def spread_piece(dims, kind, device, weights, wide_ref):
+    layers, model_dim, hidden_dim, rows, chunks = dims
+    per_row = (hidden_dim if kind == 0 else model_dim) // LANES
+    count = chunks // per_row
+    src = weights[kind]
+    slot = lax.rem(device, 4)
+
+    def spread(idx, _):
+        row = pl.multiple_of(slot * count + idx * 16, 16)
+        for layer in range(layers):
+            for col in range(per_row):
+                tile = src[layer, pl.ds(row, 16), col * LANES:(col + 1) * LANES].astype(F32)
+                base = layer + 4 * (idx * (16 * per_row) + col)
+                wide_ref[pl.ds(base, 8, stride=4 * per_row), :] = tile[0:8]
+                wide_ref[pl.ds(base + 32 * per_row, 8, stride=4 * per_row), :] = tile[8:16]
+        return 0
+
+    lax.fori_loop(0, count // 16, spread, 0)
+
+
+def mlp_block(dims, layer, w_in, w_out, hidden_ref, normed_ref, active_ref):
+    layers, model_dim, hidden_dim, rows, chunks = dims
+
+    def block(idx, _):
+        at = pl.ds(pl.multiple_of(idx * 256, 256), 256)
+        hidden = hidden_ref[at, :].astype(F32)
+        scale = lax.rsqrt(jnp.mean(hidden * hidden, axis=-1, keepdims=True) + NORM_EPS)
+        normed_ref[...] = (hidden * scale).astype(BF16)
+        for col in range(0, hidden_dim, 384):
+            inner = jnp.dot(normed_ref[...], w_in[layer, :, col:col + 384], preferred_element_type=F32).astype(BF16)
+            active_ref[:, col:col + 384] = jax.nn.gelu(inner.astype(F32), approximate=True).astype(BF16)
+        for col in range(0, model_dim, 256):
+            add = jnp.dot(active_ref[...], w_out[layer, :, col:col + 256], preferred_element_type=F32)
+            hidden_ref[at, col:col + 256] = (hidden_ref[at, col:col + 256].astype(F32) + add).astype(BF16)
+        return 0
+
+    lax.fori_loop(0, rows // 256, block, 0)
+
+
+def places():
+    me = lax.axis_index("data")
+    core = lax.rem(me, 2)
+    x_pos = lax.rem(me // 2, 2)
+    y_pos = me // 4
+    x_peer = me + 2 - 4 * x_pos
+    y_peer = me + 4 - 8 * y_pos
+    return me, core, y_pos, x_peer, y_peer, x_peer + 4 - 8 * y_pos
+
+
+def gather_kernel(dims, grad_hbm, master_hbm, one_hbm, two_hbm, tok_hbm,
+                  p0, p1, p2, p3, p4, p5, master_out, one_out, two_out, w_in, w_out, hidden_ref,
+                  grad_v, master_v, one_v, two_v,
+                  part_ref, wide_ref, normed_ref, active_ref,
                   load_sem, part_send, part_recv, send_sem, recv_sem):
     layers, model_dim, hidden_dim, rows, chunks = dims
     in_rows = chunks * LANES // hidden_dim
     out_rows = chunks * LANES // model_dim
     half_chunks = chunks // 2
 
-    me = lax.axis_index("data")
-    core = lax.rem(me, 2)
-    x_pos = lax.rem(me // 2, 2)
-    y_pos = me // 4
+    me, core, y_pos, x_peer, y_peer, diag = places()
     partner = me + 1 - 2 * core
-    x_peer = me + 2 - 4 * x_pos
-    y_peer = me + 4 - 8 * y_pos
-    diag = x_peer + 4 - 8 * y_pos
 
     state = ((grad_hbm, grad_v), (master_hbm, master_v), (one_hbm, one_v), (two_hbm, two_v))
 
@@ -51,10 +94,8 @@
     for which in range(4):
         for layer in range(layers):
             load(which, layer).start()
-    tok_load = pltpu.make_async_copy(tok_hbm, tok_v, load_sem.at[4, 0])
-    tgt_load = pltpu.make_async_copy(tgt_hbm, tgt_v, load_sem.at[4, 1])
+    tok_load = pltpu.make_async_copy(tok_hbm, hidden_ref, load_sem.at[4, 0])
     tok_load.start()
-    tgt_load.start()
 
     barrier = pltpu.get_barrier_semaphore()
     for step in range(1, GROUP):
@@ -168,29 +209,12 @@
 
             by_kind(send_own)
 
-    def pack(kind, device):
-        width = hidden_dim if kind == 0 else model_dim
-        count = in_rows if kind == 0 else out_rows
-        per_row = width // LANES
-        src = w_in if kind == 0 else w_out
-        slot = lax.rem(device, 4)
-
-        def spread(idx, _):
-            row = pl.multiple_of(slot * count + idx * 16, 16)
-            for layer in range(layers):
-                for col in range(per_row):
-                    tile = src[layer, pl.ds(row, 16), col * LANES:(col + 1) * LANES].astype(F32)
-                    base = layer + 4 * (idx * (16 * per_row) + col)
-                    wide_ref[pl.ds(base, 8, stride=4 * per_row), :] = tile[0:8]
-                    wide_ref[pl.ds(base + 32 * per_row, 8, stride=4 * per_row), :] = tile[8:16]
-            return 0
-
-        lax.fori_loop(0, count // 16, spread, 0)
+    def pack(kind, device, packed_ref):
+        spread_piece(dims, kind, device, (w_in, w_out), wide_ref)
 
         def squeeze(idx, _):
-            src_at = pl.multiple_of(idx * 128, 128)
-            block = wide_ref[pl.ds(src_at, 128), :].astype(BF16).reshape(32, 4, LANES)
-            packed_ref[pl.ds(device * chunks + idx * 32, 32), :, :] = block[:, :layers, :]
+            block = wide_ref[pl.ds(pl.multiple_of(idx * 128, 128), 128), :].astype(BF16).reshape(32, 4, LANES)
+            packed_ref[pl.ds(idx * 32, 32), :, :] = block[:, :layers, :]
             return 0
 
         lax.fori_loop(0, 4 * chunks // 128, squeeze, 0)
@@ -198,25 +222,7 @@
     def partner_of(device):
         return device + 1 - 2 * core
 
-    def mlp(layer):
-        def block(idx, _):
-            at = pl.ds(pl.multiple_of(idx * 256, 256), 256)
-            hidden = hidden_ref[at, :].astype(F32)
-            scale = lax.rsqrt(jnp.mean(hidden * hidden, axis=-1, keepdims=True) + NORM_EPS)
-            normed_ref[...] = (hidden * scale).astype(BF16)
-            for col in range(0, hidden_dim, 384):
-                inner = jnp.dot(normed_ref[...], w_in[layer, :, col:col + 384], preferred_element_type=F32).astype(BF16)
-                active_ref[:, col:col + 384] = jax.nn.gelu(inner.astype(F32), approximate=True).astype(BF16)
-            for col in range(0, model_dim, 256):
-                add = jnp.dot(active_ref[...], w_out[layer, :, col:col + 256], preferred_element_type=F32)
-                hidden_ref[at, col:col + 256] = (hidden_ref[at, col:col + 256].astype(F32) + add).astype(BF16)
-            return 0
-
-        lax.fori_loop(0, rows // 256, block, 0)
-
     tok_load.wait()
-    tgt_load.wait()
-    hidden_ref[...] = tok_v[...]
 
     for layer in range(layers):
         def forward(kind):
@@ -235,16 +241,16 @@
         by_kind(forward)
 
     def pack_near(kind):
-        pack(kind, me)
-        pack(kind, partner)
-        pack(kind, x_peer)
-        pack(1 - kind, y_peer)
+        pack(kind, me, p0)
+        pack(kind, partner, p1)
+        pack(kind, x_peer, p2)
+        pack(1 - kind, y_peer, p4)
         for layer in range(layers):
             for half in range(2):
                 copy(kind, layer, partner_of(x_peer), half, 8 + half, me).wait_recv()
                 copy(1 - kind, layer, partner_of(y_peer), half, 10 + half, me).wait_recv()
-        pack(kind, partner_of(x_peer))
-        pack(1 - kind, partner_of(y_peer))
+        pack(kind, partner_of(x_peer), p3)
+        pack(1 - kind, partner_of(y_peer), p5)
 
     by_kind(pack_near)
 
@@ -257,22 +263,8 @@
                 copy(1 - kind, layer, partner_of(diag), half, 12 + half, me).wait_recv()
 
         by_kind(far)
-        mlp(layer)
-
-    def pack_far(kind):
-        pack(1 - kind, diag)
-        pack(1 - kind, partner_of(diag))
-
-    by_kind(pack_far)
-
-    for idx in range(rows // LANES):
-        at = slice(idx * LANES, (idx + 1) * LANES)
-        error = hidden_ref[at, :].astype(F32) - tgt_v[at, :].astype(F32)
-        error = error * error
-        folded = error[:, 0:LANES]
-        for col in range(LANES, model_dim, LANES):
-            folded = folded + error[:, col:col + LANES]
-        loss_ref[idx:idx + 1, :] = jnp.sum(folded.T, axis=0, keepdims=True) * (1.0 / model_dim)
+        if layer < layers - 1:
+            mlp_block(dims, layer, w_in, w_out, hidden_ref, normed_ref, active_ref)
 
     for step in range(1, GROUP):
         part_copy(step).wait_send()
@@ -292,19 +284,51 @@
     by_kind(drain)
 
 
-def write_kernel(layers, pieces, packed_ref, master_ref, one_ref, two_ref, loss_ref,
-                 packed_hbm, master_hbm, one_hbm, two_hbm, loss_hbm, sem):
-    copies = [pltpu.make_async_copy(loss_ref, loss_hbm, sem.at[0])]
-    span = packed_ref.shape[0] // pieces
-    for idx in range(pieces):
-        at = pl.ds(idx * span, span)
-        copies.append(pltpu.make_async_copy(packed_ref.at[at], packed_hbm.at[at], sem.at[1 + idx]))
+def finish_kernel(dims, p0, p1, p2, p3, p4, p5, master_ref, one_ref, two_ref, w_in, w_out, last_ref, tgt_ref,
+                  packed_hbm, master_hbm, one_hbm, two_hbm, loss_ref,
+                  far_ref, wide_ref, normed_ref, active_ref, hidden_ref, sem, far_sem):
+    layers, model_dim, hidden_dim, rows, chunks = dims
+    me, core, y_pos, x_peer, y_peer, diag = places()
+    twin = 1 - 2 * core
+
+    copies = []
+    for idx, (ref, device) in enumerate(((p0, me), (p1, me + twin), (p2, x_peer), (p3, x_peer + twin), (p4, y_peer), (p5, y_peer + twin))):
+        copies.append(pltpu.make_async_copy(ref, packed_hbm.at[pl.ds(device * chunks, chunks)], sem.at[idx]))
     for which, (src, dst) in enumerate(((master_ref, master_hbm), (one_ref, one_hbm), (two_ref, two_hbm))):
         for layer in range(layers):
-            copies.append(pltpu.make_async_copy(src.at[layer], dst.at[:, layer, :], sem.at[1 + pieces + which * layers + layer]))
+            copies.append(pltpu.make_async_copy(src.at[layer], dst.at[:, layer, :], sem.at[6 + which * layers + layer]))
     for item in copies:
         item.start()
-    for item in copies:
+
+    far_copies = []
+    for idx, device in enumerate((diag, diag + twin)):
+        for y_value in range(2):
+            @pl.when(y_pos == y_value)
+            def _():
+                spread_piece(dims, 1 - y_value, device, (w_in, w_out), wide_ref)
+
+        def squeeze(at, _):
+            block = wide_ref[pl.ds(pl.multiple_of(at * 128, 128), 128), :].astype(BF16).reshape(32, 4, LANES)
+            far_ref[idx, pl.ds(at * 32, 32), :, :] = block[:, :layers, :]
+            return 0
+
+        lax.fori_loop(0, 4 * chunks // 128, squeeze, 0)
+        far_copies.append(pltpu.make_async_copy(far_ref.at[idx], packed_hbm.at[pl.ds(device * chunks, chunks)], far_sem.at[idx]))
+        far_copies[-1].start()
+
+    hidden_ref[...] = last_ref[...]
+    mlp_block(dims, layers - 1, w_in, w_out, hidden_ref, normed_ref, active_ref)
+
+    for idx in range(rows // LANES):
+        at = slice(idx * LANES, (idx + 1) * LANES)
+        error = hidden_ref[at, :].astype(F32) - tgt_ref[at, :].astype(F32)
+        error = error * error
+        folded = error[:, 0:LANES]
+        for col in range(LANES, model_dim, LANES):
+            folded = folded + error[:, col:col + LANES]
+        loss_ref[idx:idx + 1, :] = jnp.sum(folded.T, axis=0, keepdims=True) * (1.0 / model_dim)
+
+    for item in copies + far_copies:
         item.wait()
 
 
@@ -325,44 +349,47 @@
         hbm = pl.BlockSpec(memory_space=pltpu.HBM)
         vmem = pl.BlockSpec(memory_space=pltpu.VMEM)
         state_out = state_v
-        packed, new_master, new_one, new_two, loss = pl.pallas_call(
+        w_in_v = pltpu.VMEM((layers, model_dim, hidden_dim), BF16)
+        w_out_v = pltpu.VMEM((layers, hidden_dim, model_dim), BF16)
+        hidden_v = pltpu.VMEM((rows, model_dim), BF16)
+        wide_v = pltpu.VMEM((4 * chunks, LANES), F32)
+        normed_v = pltpu.VMEM((256, model_dim), BF16)
+        active_v = pltpu.VMEM((256, hidden_dim), BF16)
+        packed_v = pltpu.VMEM((chunks, layers, LANES), BF16)
+        gathered = pl.pallas_call(
             functools.partial(gather_kernel, dims),
             name="gather_step",
-            out_shape=(pltpu.VMEM((chunks * group_size, layers, LANES), BF16), state_out, state_out, state_out,
-                       jax.ShapeDtypeStruct((rows // LANES, LANES), F32)),
-            in_specs=[hbm] * 6,
-            out_specs=(vmem,) * 5,
+            out_shape=(*(packed_v,) * 6, state_v, state_v, state_v, w_in_v, w_out_v, hidden_v),
+            in_specs=[hbm] * 5,
+            out_specs=(vmem,) * 12,
             scratch_shapes=[
-                pltpu.VMEM((layers, model_dim, hidden_dim), BF16),
-                pltpu.VMEM((layers, hidden_dim, model_dim), BF16),
                 state_v, state_v, state_v, state_v,
-                pltpu.VMEM((rows, model_dim), BF16),
-                pltpu.VMEM((rows, model_dim), BF16),
                 pltpu.VMEM((group_size, 8, LANES), F32),
-                pltpu.VMEM((4 * chunks, LANES), F32),
-                pltpu.VMEM((256, model_dim), BF16),
-                pltpu.VMEM((256, hidden_dim), BF16),
-                pltpu.VMEM((rows, model_dim), BF16),
+                wide_v, normed_v, active_v,
                 pltpu.SemaphoreType.DMA((5, layers)),
                 pltpu.SemaphoreType.DMA((group_size,)),
                 pltpu.SemaphoreType.DMA((group_size,)),
                 pltpu.SemaphoreType.DMA((layers, 14)),
                 pltpu.SemaphoreType.DMA((layers, 14)),
             ],
-            compiler_params=pltpu.CompilerParams(collective_id=0, has_side_effects=True, vmem_limit_bytes=28 << 20),
-        )(*[pltpu.with_memory_space_constraint(a, pltpu.HBM) for a in (*tiled, tok_rows, tgt_rows)])
+            compiler_params=pltpu.CompilerParams(collective_id=0, has_side_effects=True, vmem_limit_bytes=19 << 20),
+        )(*[pltpu.with_memory_space_constraint(a, pltpu.HBM) for a in (*tiled, tok_rows)])
         state_tile = jax.ShapeDtypeStruct((chunks, layers, LANES), F32)
-        pieces = 8
         weights, new_master, new_one, new_two, row_loss = pl.pallas_call(
-            functools.partial(write_kernel, layers, pieces),
-            name="write_out",
+            functools.partial(finish_kernel, dims),
+            name="finish",
             out_shape=(jax.ShapeDtypeStruct((chunks * group_size, layers, LANES), BF16), state_tile, state_tile, state_tile,
                        jax.ShapeDtypeStruct((rows // LANES, LANES), F32)),
-            in_specs=[vmem] * 5,
-            out_specs=(hbm,) * 5,
-            scratch_shapes=[pltpu.SemaphoreType.DMA((1 + pieces + 3 * layers,))],
-            compiler_params=pltpu.CompilerParams(vmem_limit_bytes=2 << 20),
-        )(packed, new_master, new_one, new_two, loss)
+            in_specs=[vmem] * 13,
+            out_specs=(hbm, hbm, hbm, hbm, vmem),
+            scratch_shapes=[
+                pltpu.VMEM((2, chunks, layers, LANES), BF16),
+                wide_v, normed_v, active_v, hidden_v,
+                pltpu.SemaphoreType.DMA((6 + 3 * layers,)),
+                pltpu.SemaphoreType.DMA((2,)),
+            ],
+            compiler_params=pltpu.CompilerParams(vmem_limit_bytes=14 << 20),
+        )(*gathered, tgt_rows)
 
         def flat(a):
             return a.transpose(1, 0, 2).reshape(layers, a.shape[0] * LANES)

time: 74 us -> 68.2 us (0.922)
  Pallas kernels: 72.6 us -> 67.5 us
    pallas_call x1, Pallas kernels: 65 us -> 59.3 us  [local_step(): pl.pallas_call(functools.partial(gather_kernel, dims), name='gather_step'...]
where the time goes in v2:
time: 68.2 us
  Pallas kernels  67.5 us (99%)
    pallas_call x1, Pallas kernels, local_step(): pl.pallas_call(functools.partial(gather_kernel, dims), name='gather_step'...  59.3 us
    pallas_call x1, Pallas kernels, local_step(): pl.pallas_call(functools.partial(finish_kernel, dims), name='finish', out...  8.22 us

profile of v2, /device:TPU:0, one launch (start us, length us, event | category | flops | bytes accessed | tf_op | source)
XLA Modules:
  0.0 68.2 jit_solution(3797801529416320289)
XLA Ops:
  0.6 0.0 copy-start
  0.6 59.3 %gather_step.1 = (bf16[1728,3,128]{2,1,0:T(4,128)(2,1)S(1)}, bf16[1728,3,128]{2,1,0:T(4,128)(2,1)S(1)}, bf16[1728,3,128]{2,1,0:T(4,128)(2,1)S(1)}, bf16[1728,3,1...) custom-call(f32[1728,3,128]{2,1,0:T(4,128)} %bitcast.25, ...), custom_call_target="tpu_custom_call" | custom-call | tf_op jit(solution)/shard_map/gather_step/pallas_call | solution.py:359
  59.9 0.0 copy-done
  59.9 8.2 %finish.1 = (bf16[13824,3,128]{2,1,0:T(4,128)(2,1)}, f32[1728,3,128]{2,1,0:T(4,128)}, f32[1728,3,128]{2,1,0:T(4,128)}, f32[1728,3,128]{2,1,0:T(4,128)}, f32[4,128]{1,0:T(4,128)}) custom-call(bf16[1728,3,128]{2,1,0:T(4,128)(2,1)S(1)} %get-tuple-element.22.p0, bf16[1728,3,128]{2,1,0:T(4,128)(2,1)S(1)} %get-tuple-element.23.p1, ...), custom_call_target="tpu_custom_call" | custom-call | tf_op jit(solution)/shard_map/finish/pallas_call | solution.py:378
Async XLA Ops:
  0.6 59.3 %copy-start = (bf16[512,768]{1,0:T(8,128)(2,1)S(1)}, bf16[512,768]{1,0:T(8,128)(2,1)}, u32[]{:S(2)}) copy-start(bf16[512,768]{1,0:T(8,128)(2,1)} %tgt_ref.1) | copy-start | bytes 2359300

commit v3 on v2

--- a/solution.py
+++ b/solution.py
@@ -91,11 +91,9 @@
         src, dst = state[which]
         return pltpu.make_async_copy(src.at[:, layer, :], dst.at[layer], load_sem.at[which, layer])
 
-    for which in range(4):
-        for layer in range(layers):
-            load(which, layer).start()
+    for layer in range(layers):
+        load(0, layer).start()
     tok_load = pltpu.make_async_copy(tok_hbm, hidden_ref, load_sem.at[4, 0])
-    tok_load.start()
 
     barrier = pltpu.get_barrier_semaphore()
     for step in range(1, GROUP):
@@ -104,6 +102,11 @@
     sums = tuple(jnp.zeros((8, LANES), F32) for _ in range(8))
     for layer in range(layers):
         load(0, layer).wait()
+        if layer == layers - 1:
+            for item in range(layers):
+                for which in range(1, 4):
+                    load(which, item).start()
+            tok_load.start()
 
         def square(idx, carry):
             base = pl.multiple_of(idx * 64, 64)
@@ -222,7 +225,14 @@
     def partner_of(device):
         return device + 1 - 2 * core
 
-    tok_load.wait()
+    def pack_own(kind):
+        pack(kind, me, p0)
+        for layer in range(layers):
+            for half in range(2):
+                copy(kind, layer, partner, half, 6 + half, me).wait_recv()
+        pack(kind, partner, p1)
+
+    by_kind(pack_own)
 
     for layer in range(layers):
         def forward(kind):
@@ -235,36 +245,44 @@
                 if half == 1:
                     copy(1 - kind, layer, y_peer, half, 5, x_peer).start()
                 copy(1 - kind, layer, y_peer, half, 10 + half, partner).start()
-            for half in range(2):
-                copy(kind, layer, partner, half, 6 + half, me).wait_recv()
 
         by_kind(forward)
 
-    def pack_near(kind):
-        pack(kind, me, p0)
-        pack(kind, partner, p1)
+    def far_arrive(kind, layer):
+        for half in range(2):
+            copy(1 - kind, layer, diag, half, 4 + half, me).wait_recv()
+            copy(1 - kind, layer, diag, half, 12 + half, partner).start()
+
+    def far_partner(kind, layer):
+        for half in range(2):
+            copy(1 - kind, layer, partner_of(diag), half, 12 + half, me).wait_recv()
+
+    def stage_zero(kind):
         pack(kind, x_peer, p2)
         pack(1 - kind, y_peer, p4)
+        far_arrive(kind, 0)
         for layer in range(layers):
             for half in range(2):
                 copy(kind, layer, partner_of(x_peer), half, 8 + half, me).wait_recv()
                 copy(1 - kind, layer, partner_of(y_peer), half, 10 + half, me).wait_recv()
         pack(kind, partner_of(x_peer), p3)
+        far_partner(kind, 0)
+
+    def stage_one(kind):
+        far_arrive(kind, 1)
         pack(1 - kind, partner_of(y_peer), p5)
-
-    by_kind(pack_near)
-
-    for layer in range(layers):
-        def far(kind):
-            for half in range(2):
-                copy(1 - kind, layer, diag, half, 4 + half, me).wait_recv()
-                copy(1 - kind, layer, diag, half, 12 + half, partner).start()
-            for half in range(2):
-                copy(1 - kind, layer, partner_of(diag), half, 12 + half, me).wait_recv()
-
-        by_kind(far)
-        if layer < layers - 1:
-            mlp_block(dims, layer, w_in, w_out, hidden_ref, normed_ref, active_ref)
+        far_partner(kind, 1)
+
+    def stage_two(kind):
+        far_arrive(kind, 2)
+        far_partner(kind, 2)
+
+    by_kind(stage_zero)
+    tok_load.wait()
+    mlp_block(dims, 0, w_in, w_out, hidden_ref, normed_ref, active_ref)
+    by_kind(stage_one)
+    mlp_block(dims, 1, w_in, w_out, hidden_ref, normed_ref, active_ref)
+    by_kind(stage_two)
 
     for step in range(1, GROUP):
         part_copy(step).wait_send()

time: 68.2 us -> 65.1 us (0.955)
  Pallas kernels: 67.5 us -> 64.3 us
    pallas_call x1, Pallas kernels: 59.3 us -> 56.1 us  [local_step(): pl.pallas_call(functools.partial(gather_kernel, dims), name='gather_step'...]
where the time goes in v3:
time: 65.1 us; the launch traced here: 65 us
  Pallas kernels  64.3 us (99%)
  between operations  0.66 us (1%)
    pallas_call x1, Pallas kernels, local_step(): pl.pallas_call(functools.partial(gather_kernel, dims), name='gather_step'...  56.1 us
    pallas_call x1, Pallas kernels, local_step(): pl.pallas_call(functools.partial(finish_kernel, dims), name='finish', out...  8.22 us

profile of v3, /device:TPU:0, one launch (start us, length us, event | category | flops | bytes accessed | tf_op | source)
XLA Modules:
  0.0 65.0 jit_solution(13106288038621064784)
XLA Ops:
  0.6 0.0 copy-start
  0.6 56.1 %gather_step.1 = (bf16[1728,3,128]{2,1,0:T(4,128)(2,1)S(1)}, bf16[1728,3,128]{2,1,0:T(4,128)(2,1)S(1)}, bf16[1728,3,128]{2,1,0:T(4,128)(2,1)S(1)}, bf16[1728,3,1...) custom-call(f32[1728,3,128]{2,1,0:T(4,128)} %bitcast.25, ...), custom_call_target="tpu_custom_call" | custom-call | tf_op jit(solution)/shard_map/gather_step/pallas_call | solution.py:377
  56.7 0.0 copy-done
  56.7 8.2 %finish.1 = (bf16[13824,3,128]{2,1,0:T(4,128)(2,1)}, f32[1728,3,128]{2,1,0:T(4,128)}, f32[1728,3,128]{2,1,0:T(4,128)}, f32[1728,3,128]{2,1,0:T(4,128)}, f32[4,128]{1,0:T(4,128)}) custom-call(bf16[1728,3,128]{2,1,0:T(4,128)(2,1)S(1)} %get-tuple-element.22.p0, bf16[1728,3,128]{2,1,0:T(4,128)(2,1)S(1)} %get-tuple-element.23.p1, ...), custom_call_target="tpu_custom_call" | custom-call | tf_op jit(solution)/shard_map/finish/pallas_call | solution.py:396
Async XLA Ops:
  0.6 56.1 %copy-start = (bf16[512,768]{1,0:T(8,128)(2,1)S(1)}, bf16[512,768]{1,0:T(8,128)(2,1)}, u32[]{:S(2)}) copy-start(bf16[512,768]{1,0:T(8,128)(2,1)} %tgt_ref.1) | copy-start | bytes 2359300

commit v4 on v3

--- a/solution.py
+++ b/solution.py
@@ -142,17 +142,55 @@
     clip = jnp.minimum(1.0, CLIP_NORM / jnp.sqrt(total))
     clip = jnp.broadcast_to(clip, (8, LANES))
 
-    def piece(kind, layer, device, half):
-        slot = lax.rem(device, 4)
-        if kind == 0:
-            return w_in.at[layer, pl.ds(pl.multiple_of(slot * in_rows + half * (in_rows // 2), 16), in_rows // 2), :]
-        return w_out.at[layer, pl.ds(pl.multiple_of(slot * out_rows + half * (out_rows // 2), 16), out_rows // 2), :]
-
-    def copy(kind, layer, device, half, index, target):
-        ref = piece(kind, layer, device, half)
-        return pltpu.make_async_remote_copy(
-            src_ref=ref, dst_ref=ref, send_sem=send_sem.at[layer, index],
-            recv_sem=recv_sem.at[layer, index], device_id=(target,), device_id_type=MESH)
+    whole = ((0, 1),)
+    thirds = tuple((part, 3) for part in range(3))
+    slots = {}
+
+    def piece(kind, layer, device, half, part):
+        ref, count = ((w_in, in_rows), (w_out, out_rows))[kind]
+        span = count // 2 // part[1]
+        at = lax.rem(device, 4) * count + half * (count // 2) + part[0] * span
+        return ref.at[layer, pl.ds(pl.multiple_of(at, 16), span), :]
+
+    def copies(kind, layer, device, half, route, target, parts=whole):
+        out = []
+        for part in parts:
+            ref = piece(kind, layer, device, half, part)
+            index = slots.setdefault((route, layer, half, part), len(slots))
+            out.append(pltpu.make_async_remote_copy(
+                src_ref=ref, dst_ref=ref, send_sem=send_sem.at[index],
+                recv_sem=recv_sem.at[index], device_id=(target,), device_id_type=MESH))
+        return out
+
+    def start(items):
+        for item in items:
+            item.start()
+
+    def arrive(items):
+        for item in items:
+            item.wait_recv()
+
+    def left(items):
+        for item in items:
+            item.wait_send()
+
+    def own_parts(layer, half):
+        return thirds if layer == 0 and half == 0 else whole
+
+    def far_parts(layer):
+        return thirds if layer == layers - 1 else whole
+
+    def own_x(kind, layer, half, device, target, parts=None):
+        return copies(kind, layer, device, half, "own_x", target, parts or own_parts(layer, half))
+
+    def own_y(kind, layer, half, device, target, parts=None):
+        return copies(kind, layer, device, half, "own_y", target, parts or own_parts(layer, half))
+
+    def far(kind, layer, half, device, target, parts=None):
+        return copies(kind, layer, device, half, "far", target, parts or far_parts(layer))
+
+    def pair(kind, layer, half, device, route, parts=whole):
+        return copies(kind, layer, device, half, route, partner, parts)
 
     def by_kind(function):
         for y_value in range(2):
@@ -163,9 +201,11 @@
     one_scale = 1.0 / (1.0 - BETA_ONE ** ADAM_STEP)
     two_scale = 1.0 / (1.0 - BETA_TWO ** ADAM_STEP)
 
-    def adam(layer, half):
+    def adam(layer, half, part):
+        first = half * half_chunks + part[0] * (half_chunks // part[1])
+
         def update(idx, _):
-            base = pl.multiple_of(half * half_chunks + idx * 48, 8)
+            base = pl.multiple_of(first + idx * 48, 8)
             for k in range(6):
                 at = pl.ds(pl.multiple_of(base + 8 * k, 8), 8)
                 clipped = grad_v[layer, at, :] * clip
@@ -178,9 +218,9 @@
                 two_out[layer, at, :] = new_two
             return 0
 
-        lax.fori_loop(0, half_chunks // 48, update, 0)
-
-    def round_rows(kind, layer, half):
+        lax.fori_loop(0, half_chunks // part[1] // 48, update, 0)
+
+    def round_rows(kind, layer, half, part):
         width = hidden_dim if kind == 0 else model_dim
         count = in_rows if kind == 0 else out_rows
         per_row = width // LANES
@@ -188,29 +228,30 @@
         slot = lax.rem(me, 4)
 
         def body(idx, _):
-            base = half * half_chunks + idx * (16 * per_row)
-            row = pl.multiple_of(slot * count + half * (count // 2) + idx * 16, 16)
+            base = half * half_chunks + part[0] * (half_chunks // part[1]) + idx * (16 * per_row)
+            row = pl.multiple_of(slot * count + half * (count // 2) + part[0] * (count // 2 // part[1]) + idx * 16, 16)
             for col in range(per_row):
                 top = master_out[layer, pl.ds(base + col, 8, stride=per_row), :]
                 low = master_out[layer, pl.ds(base + 8 * per_row + col, 8, stride=per_row), :]
                 dst[layer, pl.ds(row, 16), col * LANES:(col + 1) * LANES] = jnp.concatenate([top, low], axis=0).astype(BF16)
             return 0
 
-        lax.fori_loop(0, count // 32, body, 0)
+        lax.fori_loop(0, count // 32 // part[1], body, 0)
 
     for layer in range(layers):
         for which in range(1, 4):
             load(which, layer).wait()
         for half in range(2):
-            adam(layer, half)
-
-            def send_own(kind):
-                round_rows(kind, layer, half)
-                copy(kind, layer, me, half, half, x_peer).start()
-                copy(kind, layer, me, half, 2 + half, y_peer).start()
-                copy(kind, layer, me, half, 6 + half, partner).start()
-
-            by_kind(send_own)
+            for part in own_parts(layer, half):
+                adam(layer, half, part)
+
+                def send_own(kind):
+                    round_rows(kind, layer, half, part)
+                    start(own_x(kind, layer, half, me, x_peer, (part,)))
+                    start(own_y(kind, layer, half, me, y_peer, (part,)))
+                    start(pair(kind, layer, half, me, "pair_own", (part,)))
+
+                by_kind(send_own)
 
     def pack(kind, device, packed_ref):
         spread_piece(dims, kind, device, (w_in, w_out), wide_ref)
@@ -229,7 +270,7 @@
         pack(kind, me, p0)
         for layer in range(layers):
             for half in range(2):
-                copy(kind, layer, partner, half, 6 + half, me).wait_recv()
+                arrive(pair(kind, layer, half, partner, "pair_own", own_parts(layer, half)))
         pack(kind, partner, p1)
 
     by_kind(pack_own)
@@ -237,25 +278,26 @@
     for layer in range(layers):
         def forward(kind):
             for half in range(2):
-                copy(kind, layer, x_peer, half, half, me).wait_recv()
+                arrive(own_x(kind, layer, half, x_peer, me))
                 if half == 0:
-                    copy(kind, layer, x_peer, half, 4, y_peer).start()
-                copy(kind, layer, x_peer, half, 8 + half, partner).start()
-                copy(1 - kind, layer, y_peer, half, 2 + half, me).wait_recv()
+                    start(far(kind, layer, half, x_peer, y_peer))
+                start(pair(kind, layer, half, x_peer, "pair_x"))
+                arrive(own_y(1 - kind, layer, half, y_peer, me))
                 if half == 1:
-                    copy(1 - kind, layer, y_peer, half, 5, x_peer).start()
-                copy(1 - kind, layer, y_peer, half, 10 + half, partner).start()
+                    start(far(1 - kind, layer, half, y_peer, x_peer))
+                start(pair(1 - kind, layer, half, y_peer, "pair_y"))
 
         by_kind(forward)
 
     def far_arrive(kind, layer):
-        for half in range(2):
-            copy(1 - kind, layer, diag, half, 4 + half, me).wait_recv()
-            copy(1 - kind, layer, diag, half, 12 + half, partner).start()
+        for part in far_parts(layer):
+            for half in range(2):
+                arrive(far(1 - kind, layer, half, diag, me, (part,)))
+                start(pair(1 - kind, layer, half, diag, "pair_far", (part,)))
 
     def far_partner(kind, layer):
         for half in range(2):
-            copy(1 - kind, layer, partner_of(diag), half, 12 + half, me).wait_recv()
+            arrive(pair(1 - kind, layer, half, partner_of(diag), "pair_far", far_parts(layer)))
 
     def stage_zero(kind):
         pack(kind, x_peer, p2)
@@ -263,8 +305,8 @@
         far_arrive(kind, 0)
         for layer in range(layers):
             for half in range(2):
-                copy(kind, layer, partner_of(x_peer), half, 8 + half, me).wait_recv()
-                copy(1 - kind, layer, partner_of(y_peer), half, 10 + half, me).wait_recv()
+                arrive(pair(kind, layer, half, partner_of(x_peer), "pair_x"))
+                arrive(pair(1 - kind, layer, half, partner_of(y_peer), "pair_y"))
         pack(kind, partner_of(x_peer), p3)
         far_partner(kind, 0)
 
@@ -290,21 +332,21 @@
     def drain(kind):
         for layer in range(layers):
             for half in range(2):
-                copy(kind, layer, me, half, half, x_peer).wait_send()
-                copy(kind, layer, me, half, 2 + half, y_peer).wait_send()
-                copy(kind, layer, me, half, 6 + half, partner).wait_send()
-                copy(kind, layer, x_peer, half, 8 + half, partner).wait_send()
-                copy(1 - kind, layer, y_peer, half, 10 + half, partner).wait_send()
-                copy(1 - kind, layer, diag, half, 12 + half, partner).wait_send()
-            copy(kind, layer, x_peer, 0, 4, y_peer).wait_send()
-            copy(1 - kind, layer, y_peer, 1, 5, x_peer).wait_send()
+                left(own_x(kind, layer, half, me, x_peer))
+                left(own_y(kind, layer, half, me, y_peer))
+                left(pair(kind, layer, half, me, "pair_own", own_parts(layer, half)))
+                left(pair(kind, layer, half, x_peer, "pair_x"))
+                left(pair(1 - kind, layer, half, y_peer, "pair_y"))
+                left(pair(1 - kind, layer, half, diag, "pair_far", far_parts(layer)))
+            left(far(kind, layer, 0, x_peer, y_peer))
+            left(far(1 - kind, layer, 1, y_peer, x_peer))
 
     by_kind(drain)
 
 
 def finish_kernel(dims, p0, p1, p2, p3, p4, p5, master_ref, one_ref, two_ref, w_in, w_out, last_ref, tgt_ref,
-                  packed_hbm, master_hbm, one_hbm, two_hbm, loss_ref,
-                  far_ref, wide_ref, normed_ref, active_ref, hidden_ref, sem, far_sem):
+                  packed_hbm, master_hbm, one_hbm, two_hbm, loss_hbm,
+                  loss_ref, far_ref, wide_ref, normed_ref, active_ref, hidden_ref, sem, far_sem):
     layers, model_dim, hidden_dim, rows, chunks = dims
     me, core, y_pos, x_peer, y_peer, diag = places()
     twin = 1 - 2 * core
@@ -346,7 +388,9 @@
             folded = folded + error[:, col:col + LANES]
         loss_ref[idx:idx + 1, :] = jnp.sum(folded.T, axis=0, keepdims=True) * (1.0 / model_dim)
 
-    for item in copies + far_copies:
+    loss_copy = pltpu.make_async_copy(loss_ref, loss_hbm, far_sem.at[2])
+    loss_copy.start()
+    for item in copies + far_copies + [loss_copy]:
         item.wait()
 
 
@@ -387,8 +431,8 @@
                 pltpu.SemaphoreType.DMA((5, layers)),
                 pltpu.SemaphoreType.DMA((group_size,)),
                 pltpu.SemaphoreType.DMA((group_size,)),
-                pltpu.SemaphoreType.DMA((layers, 14)),
-                pltpu.SemaphoreType.DMA((layers, 14)),
+                pltpu.SemaphoreType.DMA((96,)),
+                pltpu.SemaphoreType.DMA((96,)),
             ],
             compiler_params=pltpu.CompilerParams(collective_id=0, has_side_effects=True, vmem_limit_bytes=19 << 20),
         )(*[pltpu.with_memory_space_constraint(a, pltpu.HBM) for a in (*tiled, tok_rows)])
@@ -399,12 +443,13 @@
             out_shape=(jax.ShapeDtypeStruct((chunks * group_size, layers, LANES), BF16), state_tile, state_tile, state_tile,
                        jax.ShapeDtypeStruct((rows // LANES, LANES), F32)),
             in_specs=[vmem] * 13,
-            out_specs=(hbm, hbm, hbm, hbm, vmem),
+            out_specs=(hbm,) * 5,
             scratch_shapes=[
+                pltpu.VMEM((rows // LANES, LANES), F32),
                 pltpu.VMEM((2, chunks, layers, LANES), BF16),
                 wide_v, normed_v, active_v, hidden_v,
                 pltpu.SemaphoreType.DMA((6 + 3 * layers,)),
-                pltpu.SemaphoreType.DMA((2,)),
+                pltpu.SemaphoreType.DMA((3,)),
             ],
             compiler_params=pltpu.CompilerParams(vmem_limit_bytes=14 << 20),
         )(*gathered, tgt_rows)

time: 65.1 us -> 65 us (level)
  no operation moved by 1% of the time
where the time goes in v4:
time: 65 us; the launch traced here: 64.9 us
  Pallas kernels  64.2 us (99%)
  between operations  0.66 us (1%)
    pallas_call x1, Pallas kernels, local_step(): pl.pallas_call(functools.partial(gather_kernel, dims), name='gather_step'...  56.6 us
    pallas_call x1, Pallas kernels, local_step(): pl.pallas_call(functools.partial(finish_kernel, dims), name='finish', out...  7.65 us

profile of v4, /device:TPU:0, one launch (start us, length us, event | category | flops | bytes accessed | tf_op | source)
XLA Modules:
  0.0 64.9 jit_solution(13431311849839761185)
XLA Ops:
  0.6 0.0 copy-start
  0.6 56.6 %gather_step.1 = (bf16[1728,3,128]{2,1,0:T(4,128)(2,1)S(1)}, bf16[1728,3,128]{2,1,0:T(4,128)(2,1)S(1)}, bf16[1728,3,128]{2,1,0:T(4,128)(2,1)S(1)}, bf16[1728,3,1...) custom-call(f32[1728,3,128]{2,1,0:T(4,128)} %bitcast.25, ...), custom_call_target="tpu_custom_call" | custom-call | tf_op jit(solution)/shard_map/gather_step/pallas_call | solution.py:421
  57.2 0.0 copy-done
  57.2 7.6 %finish.1 = (bf16[13824,3,128]{2,1,0:T(4,128)(2,1)}, f32[1728,3,128]{2,1,0:T(4,128)}, f32[1728,3,128]{2,1,0:T(4,128)}, f32[1728,3,128]{2,1,0:T(4,128)}, f32[4,128]{1,0:T(4,128)}) custom-call(bf16[1728,3,128]{2,1,0:T(4,128)(2,1)S(1)} %get-tuple-element.22.p0, bf16[1728,3,128]{2,1,0:T(4,128)(2,1)S(1)} %get-tuple-element.23.p1, ...), custom_call_target="tpu_custom_call" | custom-call | tf_op jit(solution)/shard_map/finish/pallas_call | solution.py:440
Async XLA Ops:
  0.6 56.6 %copy-start = (bf16[512,768]{1,0:T(8,128)(2,1)S(1)}, bf16[512,768]{1,0:T(8,128)(2,1)}, u32[]{:S(2)}) copy-start(bf16[512,768]{1,0:T(8,128)(2,1)} %tgt_ref.1) | copy-start | bytes 2359300

commit v5 on v4

--- a/solution.py
+++ b/solution.py
@@ -80,7 +80,6 @@
     layers, model_dim, hidden_dim, rows, chunks = dims
     in_rows = chunks * LANES // hidden_dim
     out_rows = chunks * LANES // model_dim
-    half_chunks = chunks // 2
 
     me, core, y_pos, x_peer, y_peer, diag = places()
     partner = me + 1 - 2 * core
@@ -142,21 +141,19 @@
     clip = jnp.minimum(1.0, CLIP_NORM / jnp.sqrt(total))
     clip = jnp.broadcast_to(clip, (8, LANES))
 
-    whole = ((0, 1),)
-    thirds = tuple((part, 3) for part in range(3))
     slots = {}
 
-    def piece(kind, layer, device, half, part):
+    def piece(kind, layer, device, part):
         ref, count = ((w_in, in_rows), (w_out, out_rows))[kind]
-        span = count // 2 // part[1]
-        at = lax.rem(device, 4) * count + half * (count // 2) + part[0] * span
+        span = count // part[1]
+        at = lax.rem(device, 4) * count + part[0] * span
         return ref.at[layer, pl.ds(pl.multiple_of(at, 16), span), :]
 
-    def copies(kind, layer, device, half, route, target, parts=whole):
+    def copies(kind, layer, device, route, target, parts):
         out = []
         for part in parts:
-            ref = piece(kind, layer, device, half, part)
-            index = slots.setdefault((route, layer, half, part), len(slots))
+            ref = piece(kind, layer, device, part)
+            index = slots.setdefault((route, layer, part), len(slots))
             out.append(pltpu.make_async_remote_copy(
                 src_ref=ref, dst_ref=ref, send_sem=send_sem.at[index],
                 recv_sem=recv_sem.at[index], device_id=(target,), device_id_type=MESH))
@@ -174,23 +171,22 @@
         for item in items:
             item.wait_send()
 
-    def own_parts(layer, half):
-        return thirds if layer == 0 and half == 0 else whole
-
-    def far_parts(layer):
-        return thirds if layer == layers - 1 else whole
-
-    def own_x(kind, layer, half, device, target, parts=None):
-        return copies(kind, layer, device, half, "own_x", target, parts or own_parts(layer, half))
-
-    def own_y(kind, layer, half, device, target, parts=None):
-        return copies(kind, layer, device, half, "own_y", target, parts or own_parts(layer, half))
-
-    def far(kind, layer, half, device, target, parts=None):
-        return copies(kind, layer, device, half, "far", target, parts or far_parts(layer))
-
-    def pair(kind, layer, half, device, route, parts=whole):
-        return copies(kind, layer, device, half, route, partner, parts)
+    def own_parts(layer):
+        return ((0, 2), (1, 2))
+
+    def own_x(kind, layer, device, target, parts=None):
+        return copies(kind, layer, device, "own_x", target, parts or own_parts(layer))
+
+    def own_y(kind, layer, device, target, parts=None):
+        return copies(kind, layer, device, "own_y", target, parts or own_parts(layer))
+
+    def far(kind, layer, half, device, target):
+        return copies(kind, layer, device, "far", target, ((half, 2),))
+
+    def pair(kind, layer, device, route, parts):
+        return copies(kind, layer, device, route, partner, parts)
+
+    HALVES = ((0, 2), (1, 2))
 
     def by_kind(function):
         for y_value in range(2):
@@ -201,8 +197,8 @@
     one_scale = 1.0 / (1.0 - BETA_ONE ** ADAM_STEP)
     two_scale = 1.0 / (1.0 - BETA_TWO ** ADAM_STEP)
 
-    def adam(layer, half, part):
-        first = half * half_chunks + part[0] * (half_chunks // part[1])
+    def adam(layer, part):
+        first = part[0] * (chunks // part[1])
 
         def update(idx, _):
             base = pl.multiple_of(first + idx * 48, 8)
@@ -218,9 +214,9 @@
                 two_out[layer, at, :] = new_two
             return 0
 
-        lax.fori_loop(0, half_chunks // part[1] // 48, update, 0)
-
-    def round_rows(kind, layer, half, part):
+        lax.fori_loop(0, chunks // part[1] // 48, update, 0)
+
+    def round_rows(kind, layer, part):
         width = hidden_dim if kind == 0 else model_dim
         count = in_rows if kind == 0 else out_rows
         per_row = width // LANES
@@ -228,40 +224,39 @@
         slot = lax.rem(me, 4)
 
         def body(idx, _):
-            base = half * half_chunks + part[0] * (half_chunks // part[1]) + idx * (16 * per_row)
-            row = pl.multiple_of(slot * count + half * (count // 2) + part[0] * (count // 2 // part[1]) + idx * 16, 16)
+            base = part[0] * (chunks // part[1]) + idx * (16 * per_row)
+            row = pl.multiple_of(slot * count + part[0] * (count // part[1]) + idx * 16, 16)
             for col in range(per_row):
                 top = master_out[layer, pl.ds(base + col, 8, stride=per_row), :]
                 low = master_out[layer, pl.ds(base + 8 * per_row + col, 8, stride=per_row), :]
                 dst[layer, pl.ds(row, 16), col * LANES:(col + 1) * LANES] = jnp.concatenate([top, low], axis=0).astype(BF16)
             return 0
 
-        lax.fori_loop(0, count // 32 // part[1], body, 0)
+        lax.fori_loop(0, count // 16 // part[1], body, 0)
 
     for layer in range(layers):
         for which in range(1, 4):
             load(which, layer).wait()
-        for half in range(2):
-            for part in own_parts(layer, half):
-                adam(layer, half, part)
-
-                def send_own(kind):
-                    round_rows(kind, layer, half, part)
-                    start(own_x(kind, layer, half, me, x_peer, (part,)))
-                    start(own_y(kind, layer, half, me, y_peer, (part,)))
-                    start(pair(kind, layer, half, me, "pair_own", (part,)))
-
-                by_kind(send_own)
+        for part in own_parts(layer):
+            adam(layer, part)
+
+            def send_own(kind):
+                round_rows(kind, layer, part)
+                start(own_x(kind, layer, me, x_peer, (part,)))
+                start(own_y(kind, layer, me, y_peer, (part,)))
+                start(pair(kind, layer, me, "pair_own", (part,)))
+
+            by_kind(send_own)
 
     def pack(kind, device, packed_ref):
         spread_piece(dims, kind, device, (w_in, w_out), wide_ref)
 
         def squeeze(idx, _):
-            block = wide_ref[pl.ds(pl.multiple_of(idx * 128, 128), 128), :].astype(BF16).reshape(32, 4, LANES)
-            packed_ref[pl.ds(idx * 32, 32), :, :] = block[:, :layers, :]
+            at = pl.ds(pl.multiple_of(idx * 256, 256), 256)
+            packed_ref[at, :] = wide_ref[at, :].astype(BF16)
             return 0
 
-        lax.fori_loop(0, 4 * chunks // 128, squeeze, 0)
+        lax.fori_loop(0, 4 * chunks // 256, squeeze, 0)
 
     def partner_of(device):
         return device + 1 - 2 * core
@@ -269,50 +264,47 @@
     def pack_own(kind):
         pack(kind, me, p0)
         for layer in range(layers):
-            for half in range(2):
-                arrive(pair(kind, layer, half, partner, "pair_own", own_parts(layer, half)))
+            arrive(pair(kind, layer, partner, "pair_own", own_parts(layer)))
         pack(kind, partner, p1)
 
     by_kind(pack_own)
 
     for layer in range(layers):
         def forward(kind):
-            for half in range(2):
-                arrive(own_x(kind, layer, half, x_peer, me))
-                if half == 0:
-                    start(far(kind, layer, half, x_peer, y_peer))
-                start(pair(kind, layer, half, x_peer, "pair_x"))
-                arrive(own_y(1 - kind, layer, half, y_peer, me))
-                if half == 1:
-                    start(far(1 - kind, layer, half, y_peer, x_peer))
-                start(pair(1 - kind, layer, half, y_peer, "pair_y"))
+            for at, part in enumerate(own_parts(layer)):
+                last = at == len(own_parts(layer)) - 1
+                arrive(own_x(kind, layer, x_peer, me, (part,)))
+                if at == 0:
+                    start(far(kind, layer, 0, x_peer, y_peer))
+                start(pair(kind, layer, x_peer, "pair_x", (part,)))
+                arrive(own_y(1 - kind, layer, y_peer, me, (part,)))
+                if last:
+                    start(far(1 - kind, layer, 1, y_peer, x_peer))
+                start(pair(1 - kind, layer, y_peer, "pair_y", (part,)))
 
         by_kind(forward)
 
     def far_arrive(kind, layer):
-        for part in far_parts(layer):
-            for half in range(2):
-                arrive(far(1 - kind, layer, half, diag, me, (part,)))
-                start(pair(1 - kind, layer, half, diag, "pair_far", (part,)))
+        for half in range(2):
+            arrive(far(1 - kind, layer, half, diag, me))
+            start(pair(1 - kind, layer, diag, "pair_far", ((half, 2),)))
 
     def far_partner(kind, layer):
-        for half in range(2):
-            arrive(pair(1 - kind, layer, half, partner_of(diag), "pair_far", far_parts(layer)))
+        arrive(pair(1 - kind, layer, partner_of(diag), "pair_far", HALVES))
 
     def stage_zero(kind):
         pack(kind, x_peer, p2)
         pack(1 - kind, y_peer, p4)
+        for layer in range(layers):
+            arrive(pair(kind, layer, partner_of(x_peer), "pair_x", own_parts(layer)))
+            arrive(pair(1 - kind, layer, partner_of(y_peer), "pair_y", own_parts(layer)))
+        pack(kind, partner_of(x_peer), p3)
+        pack(1 - kind, partner_of(y_peer), p5)
         far_arrive(kind, 0)
-        for layer in range(layers):
-            for half in range(2):
-                arrive(pair(kind, layer, half, partner_of(x_peer), "pair_x"))
-                arrive(pair(1 - kind, layer, half, partner_of(y_peer), "pair_y"))
-        pack(kind, partner_of(x_peer), p3)
         far_partner(kind, 0)
 
     def stage_one(kind):
         far_arrive(kind, 1)
-        pack(1 - kind, partner_of(y_peer), p5)
         far_partner(kind, 1)
 
     def stage_two(kind):
@@ -331,13 +323,12 @@
 
     def drain(kind):
         for layer in range(layers):
-            for half in range(2):
-                left(own_x(kind, layer, half, me, x_peer))
-                left(own_y(kind, layer, half, me, y_peer))
-                left(pair(kind, layer, half, me, "pair_own", own_parts(layer, half)))
-                left(pair(kind, layer, half, x_peer, "pair_x"))
-                left(pair(1 - kind, layer, half, y_peer, "pair_y"))
-                left(pair(1 - kind, layer, half, diag, "pair_far", far_parts(layer)))
+            left(own_x(kind, layer, me, x_peer))
+            left(own_y(kind, layer, me, y_peer))
+            left(pair(kind, layer, me, "pair_own", own_parts(layer)))
+            left(pair(kind, layer, x_peer, "pair_x", own_parts(layer)))
+            left(pair(1 - kind, layer, y_peer, "pair_y", own_parts(layer)))
+            left(pair(1 - kind, layer, diag, "pair_far", HALVES))
             left(far(kind, layer, 0, x_peer, y_peer))
             left(far(1 - kind, layer, 1, y_peer, x_peer))
 
@@ -417,7 +408,7 @@
         wide_v = pltpu.VMEM((4 * chunks, LANES), F32)
         normed_v = pltpu.VMEM((256, model_dim), BF16)
         active_v = pltpu.VMEM((256, hidden_dim), BF16)
-        packed_v = pltpu.VMEM((chunks, layers, LANES), BF16)
+        packed_v = pltpu.VMEM((4 * chunks, LANES), BF16)
         gathered = pl.pallas_call(
             functools.partial(gather_kernel, dims),
             name="gather_step",
@@ -436,6 +427,7 @@
             ],
             compiler_params=pltpu.CompilerParams(collective_id=0, has_side_effects=True, vmem_limit_bytes=19 << 20),
         )(*[pltpu.with_memory_space_constraint(a, pltpu.HBM) for a in (*tiled, tok_rows)])
+        gathered = [a.reshape(chunks, 4, LANES)[:, :layers, :] for a in gathered[:6]] + list(gathered[6:])
         state_tile = jax.ShapeDtypeStruct((chunks, layers, LANES), F32)
         weights, new_master, new_one, new_two, row_loss = pl.pallas_call(
             functools.partial(finish_kernel, dims),

time: 65 us -> 65.5 us (level)
  no operation moved by 1% of the time
where the time goes in v5:
time: 65.5 us; the launch traced here: 65.3 us
  Pallas kernels  64.7 us (99%)
  between operations  0.66 us (1%)
    pallas_call x1, Pallas kernels, local_step(): pl.pallas_call(functools.partial(gather_kernel, dims), name='gather_step'...  57 us
    pallas_call x1, Pallas kernels, local_step(): pl.pallas_call(functools.partial(finish_kernel, dims), name='finish', out...  7.65 us

profile of v5, /device:TPU:0, one launch (start us, length us, event | category | flops | bytes accessed | tf_op | source)
XLA Modules:
  0.0 65.3 jit_solution(16262330640906118885)
XLA Ops:
  0.6 0.0 copy-start
  0.6 57.0 %gather_step.1 = (bf16[6912,128]{1,0:T(8,128)(2,1)S(1)}, bf16[6912,128]{1,0:T(8,128)(2,1)S(1)}, bf16[6912,128]{1,0:T(8,128)(2,1)S(1)}, bf16[6912,128]{1,0:T(8,12...) custom-call(f32[1728,3,128]{2,1,0:T(4,128)} %bitcast.43, ...), custom_call_target="tpu_custom_call" | custom-call | tf_op jit(solution)/shard_map/gather_step/pallas_call | solution.py:412
  57.7 0.0 copy-done
  57.7 7.6 %finish.1 = (bf16[13824,3,128]{2,1,0:T(4,128)(2,1)}, f32[1728,3,128]{2,1,0:T(4,128)}, f32[1728,3,128]{2,1,0:T(4,128)}, f32[1728,3,128]{2,1,0:T(4,128)}, f32[4,128]{1,0:T(4,128)}) custom-call(bf16[1728,3,128]{2,1,0:T(4,128)(2,1)S(1)} %bitcast.37, bf16[1728,3,128]{2,1,0:T(4,128)(2,1)S(1)} %bitcast.38, bf16[1728,3,128]{2,1,0:T(4,128)(2,1)S(1)} %bitcast.39, ...), custom_call_target="tpu_custom_call" | custom-call | tf_op jit(solution)/shard_map/finish/pallas_call | solution.py:432
Async XLA Ops:
  0.6 57.1 %copy-start = (bf16[512,768]{1,0:T(8,128)(2,1)S(1)}, bf16[512,768]{1,0:T(8,128)(2,1)}, u32[]{:S(2)}) copy-start(bf16[512,768]{1,0:T(8,128)(2,1)} %tgt_ref.1) | copy-start | bytes 2359300

commit v6 on v5

--- a/solution.py
+++ b/solution.py
@@ -172,7 +172,10 @@
             item.wait_send()
 
     def own_parts(layer):
-        return ((0, 2), (1, 2))
+        return ((0, 6), (1, 6), (2, 6), (1, 2)) if layer == 0 else ((0, 2), (1, 2))
+
+    def far_parts(layer, half):
+        return tuple((3 * half + at, 6) for at in range(3)) if layer == layers - 1 else ((half, 2),)
 
     def own_x(kind, layer, device, target, parts=None):
         return copies(kind, layer, device, "own_x", target, parts or own_parts(layer))
@@ -180,13 +183,11 @@
     def own_y(kind, layer, device, target, parts=None):
         return copies(kind, layer, device, "own_y", target, parts or own_parts(layer))
 
-    def far(kind, layer, half, device, target):
-        return copies(kind, layer, device, "far", target, ((half, 2),))
+    def far(kind, layer, half, device, target, parts=None):
+        return copies(kind, layer, device, "far", target, parts or far_parts(layer, half))
 
     def pair(kind, layer, device, route, parts):
         return copies(kind, layer, device, route, partner, parts)
-
-    HALVES = ((0, 2), (1, 2))
 
     def by_kind(function):
         for y_value in range(2):
@@ -242,8 +243,9 @@
 
             def send_own(kind):
                 round_rows(kind, layer, part)
-                start(own_x(kind, layer, me, x_peer, (part,)))
-                start(own_y(kind, layer, me, y_peer, (part,)))
+                if layer < layers - 1:
+                    start(own_x(kind, layer, me, x_peer, (part,)))
+                    start(own_y(kind, layer, me, y_peer, (part,)))
                 start(pair(kind, layer, me, "pair_own", (part,)))
 
             by_kind(send_own)
@@ -261,46 +263,44 @@
     def partner_of(device):
         return device + 1 - 2 * core
 
-    def pack_own(kind):
+    def forward(kind, layer):
+        x_order = own_parts(layer)
+        y_order = x_order[::-1] if layer == layers - 1 else x_order
+        for x_part, y_part in zip(x_order, y_order):
+            arrive(own_x(kind, layer, x_peer, me, (x_part,)))
+            if x_part in ((0, 2), (2, 6)):
+                start(far(kind, layer, 0, x_peer, y_peer))
+            start(pair(kind, layer, x_peer, "pair_x", (x_part,)))
+            arrive(own_y(1 - kind, layer, y_peer, me, (y_part,)))
+            if y_part == (1, 2):
+                start(far(1 - kind, layer, 1, y_peer, x_peer))
+            start(pair(1 - kind, layer, y_peer, "pair_y", (y_part,)))
+
+    def far_arrive(kind, layer):
+        for parts in zip(far_parts(layer, 0), far_parts(layer, 1)):
+            for half in range(2):
+                arrive(far(1 - kind, layer, half, diag, me, (parts[half],)))
+                start(pair(1 - kind, layer, diag, "pair_far", (parts[half],)))
+
+    def far_partner(kind, layer):
+        arrive(pair(1 - kind, layer, partner_of(diag), "pair_far", far_parts(layer, 0) + far_parts(layer, 1)))
+
+    def near_partner(kind, layer):
+        arrive(pair(kind, layer, partner_of(x_peer), "pair_x", own_parts(layer)))
+        arrive(pair(1 - kind, layer, partner_of(y_peer), "pair_y", own_parts(layer)))
+
+    def stage_own(kind):
         pack(kind, me, p0)
+        forward(kind, 0)
         for layer in range(layers):
             arrive(pair(kind, layer, partner, "pair_own", own_parts(layer)))
         pack(kind, partner, p1)
-
-    by_kind(pack_own)
-
-    for layer in range(layers):
-        def forward(kind):
-            for at, part in enumerate(own_parts(layer)):
-                last = at == len(own_parts(layer)) - 1
-                arrive(own_x(kind, layer, x_peer, me, (part,)))
-                if at == 0:
-                    start(far(kind, layer, 0, x_peer, y_peer))
-                start(pair(kind, layer, x_peer, "pair_x", (part,)))
-                arrive(own_y(1 - kind, layer, y_peer, me, (part,)))
-                if last:
-                    start(far(1 - kind, layer, 1, y_peer, x_peer))
-                start(pair(1 - kind, layer, y_peer, "pair_y", (part,)))
-
-        by_kind(forward)
-
-    def far_arrive(kind, layer):
-        for half in range(2):
-            arrive(far(1 - kind, layer, half, diag, me))
-            start(pair(1 - kind, layer, diag, "pair_far", ((half, 2),)))
-
-    def far_partner(kind, layer):
-        arrive(pair(1 - kind, layer, partner_of(diag), "pair_far", HALVES))
-
-    def stage_zero(kind):
-        pack(kind, x_peer, p2)
-        pack(1 - kind, y_peer, p4)
-        for layer in range(layers):
-            arrive(pair(kind, layer, partner_of(x_peer), "pair_x", own_parts(layer)))
-            arrive(pair(1 - kind, layer, partner_of(y_peer), "pair_y", own_parts(layer)))
-        pack(kind, partner_of(x_peer), p3)
-        pack(1 - kind, partner_of(y_peer), p5)
+        forward(kind, 1)
+        start(own_x(kind, layers - 1, me, x_peer))
+        start(own_y(kind, layers - 1, me, y_peer)[::-1])
+        near_partner(kind, 0)
         far_arrive(kind, 0)
+        near_partner(kind, 1)
         far_partner(kind, 0)
 
     def stage_one(kind):
@@ -308,10 +308,16 @@
         far_partner(kind, 1)
 
     def stage_two(kind):
+        forward(kind, 2)
+        pack(kind, x_peer, p2)
+        pack(1 - kind, y_peer, p4)
+        near_partner(kind, 2)
+        pack(kind, partner_of(x_peer), p3)
+        pack(1 - kind, partner_of(y_peer), p5)
         far_arrive(kind, 2)
         far_partner(kind, 2)
 
-    by_kind(stage_zero)
+    by_kind(stage_own)
     tok_load.wait()
     mlp_block(dims, 0, w_in, w_out, hidden_ref, normed_ref, active_ref)
     by_kind(stage_one)
@@ -328,7 +334,7 @@
             left(pair(kind, layer, me, "pair_own", own_parts(layer)))
             left(pair(kind, layer, x_peer, "pair_x", own_parts(layer)))
             left(pair(1 - kind, layer, y_peer, "pair_y", own_parts(layer)))
-            left(pair(1 - kind, layer, diag, "pair_far", HALVES))
+            left(pair(1 - kind, layer, diag, "pair_far", far_parts(layer, 0) + far_parts(layer, 1)))
             left(far(kind, layer, 0, x_peer, y_peer))
             left(far(1 - kind, layer, 1, y_peer, x_peer))
 

time: 65.5 us -> 63.9 us (0.976)
  Pallas kernels: 64.7 us -> 63.1 us
    pallas_call x1, Pallas kernels: 57 us -> 55.5 us  [local_step(): pl.pallas_call(functools.partial(gather_kernel, dims), name='gather_step'...]
where the time goes in v6:
time: 63.9 us; the launch traced here: 63.8 us
  Pallas kernels  63.1 us (99%)
  between operations  0.66 us (1%)
    pallas_call x1, Pallas kernels, local_step(): pl.pallas_call(functools.partial(gather_kernel, dims), name='gather_step'...  55.5 us
    pallas_call x1, Pallas kernels, local_step(): pl.pallas_call(functools.partial(finish_kernel, dims), name='finish', out...  7.65 us

profile of v6, /device:TPU:0, one launch (start us, length us, event | category | flops | bytes accessed | tf_op | source)
XLA Modules:
  0.0 63.8 jit_solution(15341952281488190936)
XLA Ops:
  0.6 0.0 copy-start
  0.6 55.5 %gather_step.1 = (bf16[6912,128]{1,0:T(8,128)(2,1)S(1)}, bf16[6912,128]{1,0:T(8,128)(2,1)S(1)}, bf16[6912,128]{1,0:T(8,128)(2,1)S(1)}, bf16[6912,128]{1,0:T(8,12...) custom-call(f32[1728,3,128]{2,1,0:T(4,128)} %bitcast.43, ...), custom_call_target="tpu_custom_call" | custom-call | tf_op jit(solution)/shard_map/gather_step/pallas_call | solution.py:418
  56.1 0.0 copy-done
  56.1 7.6 %finish.1 = (bf16[13824,3,128]{2,1,0:T(4,128)(2,1)}, f32[1728,3,128]{2,1,0:T(4,128)}, f32[1728,3,128]{2,1,0:T(4,128)}, f32[1728,3,128]{2,1,0:T(4,128)}, f32[4,128]{1,0:T(4,128)}) custom-call(bf16[1728,3,128]{2,1,0:T(4,128)(2,1)S(1)} %bitcast.37, bf16[1728,3,128]{2,1,0:T(4,128)(2,1)S(1)} %bitcast.38, bf16[1728,3,128]{2,1,0:T(4,128)(2,1)S(1)} %bitcast.39, ...), custom_call_target="tpu_custom_call" | custom-call | tf_op jit(solution)/shard_map/finish/pallas_call | solution.py:438
Async XLA Ops:
  0.6 55.5 %copy-start = (bf16[512,768]{1,0:T(8,128)(2,1)S(1)}, bf16[512,768]{1,0:T(8,128)(2,1)}, u32[]{:S(2)}) copy-start(bf16[512,768]{1,0:T(8,128)(2,1)} %tgt_ref.1) | copy-start | bytes 2359300

commit v7 on v6

--- a/solution.py
+++ b/solution.py
@@ -102,10 +102,8 @@
     for layer in range(layers):
         load(0, layer).wait()
         if layer == layers - 1:
-            for item in range(layers):
-                for which in range(1, 4):
-                    load(which, item).start()
-            tok_load.start()
+            for which in range(1, 4):
+                load(which, 0).start()
 
         def square(idx, carry):
             base = pl.multiple_of(idx * 64, 64)
@@ -132,6 +130,10 @@
 
     for step in range(1, GROUP):
         part_copy(step).start()
+    for item in range(1, layers):
+        for which in range(1, 4):
+            load(which, item).start()
+    tok_load.start()
     for step in range(1, GROUP):
         part_arrival(step).wait_recv()
     total = part_ref[0]
@@ -276,8 +278,10 @@
                 start(far(1 - kind, layer, 1, y_peer, x_peer))
             start(pair(1 - kind, layer, y_peer, "pair_y", (y_part,)))
 
-    def far_arrive(kind, layer):
-        for parts in zip(far_parts(layer, 0), far_parts(layer, 1)):
+    def far_arrive(kind, layer, only=None):
+        for idx, parts in enumerate(zip(far_parts(layer, 0), far_parts(layer, 1))):
+            if only is not None and idx != only:
+                continue
             for half in range(2):
                 arrive(far(1 - kind, layer, half, diag, me, (parts[half],)))
                 start(pair(1 - kind, layer, diag, "pair_far", (parts[half],)))
@@ -312,9 +316,11 @@
         pack(kind, x_peer, p2)
         pack(1 - kind, y_peer, p4)
         near_partner(kind, 2)
+        far_arrive(kind, 2, 0)
         pack(kind, partner_of(x_peer), p3)
+        far_arrive(kind, 2, 1)
         pack(1 - kind, partner_of(y_peer), p5)
-        far_arrive(kind, 2)
+        far_arrive(kind, 2, 2)
         far_partner(kind, 2)
 
     by_kind(stage_own)

time: 63.9 us -> 63.9 us (level)
  no operation moved by 1% of the time
where the time goes in v7:
time: 63.9 us; the launch traced here: 63.8 us
  Pallas kernels  63.1 us (99%)
  between operations  0.66 us (1%)
    pallas_call x1, Pallas kernels, local_step(): pl.pallas_call(functools.partial(gather_kernel, dims), name='gather_step'...  55.5 us
    pallas_call x1, Pallas kernels, local_step(): pl.pallas_call(functools.partial(finish_kernel, dims), name='finish', out...  7.65 us

profile of v7, /device:TPU:0, one launch (start us, length us, event | category | flops | bytes accessed | tf_op | source)
XLA Modules:
  0.0 63.8 jit_solution(16245520434087642892)
XLA Ops:
  0.6 0.0 copy-start
  0.6 55.5 %gather_step.1 = (bf16[6912,128]{1,0:T(8,128)(2,1)S(1)}, bf16[6912,128]{1,0:T(8,128)(2,1)S(1)}, bf16[6912,128]{1,0:T(8,128)(2,1)S(1)}, bf16[6912,128]{1,0:T(8,12...) custom-call(f32[1728,3,128]{2,1,0:T(4,128)} %bitcast.43, ...), custom_call_target="tpu_custom_call" | custom-call | tf_op jit(solution)/shard_map/gather_step/pallas_call | solution.py:424
  56.1 0.0 copy-done
  56.1 7.6 %finish.1 = (bf16[13824,3,128]{2,1,0:T(4,128)(2,1)}, f32[1728,3,128]{2,1,0:T(4,128)}, f32[1728,3,128]{2,1,0:T(4,128)}, f32[1728,3,128]{2,1,0:T(4,128)}, f32[4,128]{1,0:T(4,128)}) custom-call(bf16[1728,3,128]{2,1,0:T(4,128)(2,1)S(1)} %bitcast.37, bf16[1728,3,128]{2,1,0:T(4,128)(2,1)S(1)} %bitcast.38, bf16[1728,3,128]{2,1,0:T(4,128)(2,1)S(1)} %bitcast.39, ...), custom_call_target="tpu_custom_call" | custom-call | tf_op jit(solution)/shard_map/finish/pallas_call | solution.py:444
Async XLA Ops:
  0.6 55.5 %copy-start = (bf16[512,768]{1,0:T(8,128)(2,1)S(1)}, bf16[512,768]{1,0:T(8,128)(2,1)}, u32[]{:S(2)}) copy-start(bf16[512,768]{1,0:T(8,128)(2,1)} %tgt_ref.1) | copy-start | bytes 2359300

commit v8 on v7

--- a/solution.py
+++ b/solution.py
@@ -174,10 +174,10 @@
             item.wait_send()
 
     def own_parts(layer):
-        return ((0, 6), (1, 6), (2, 6), (1, 2)) if layer == 0 else ((0, 2), (1, 2))
+        return ((0, 1),) if layer == 1 else ((0, 2), (1, 2))
 
     def far_parts(layer, half):
-        return tuple((3 * half + at, 6) for at in range(3)) if layer == layers - 1 else ((half, 2),)
+        return ((half, 2),)
 
     def own_x(kind, layer, device, target, parts=None):
         return copies(kind, layer, device, "own_x", target, parts or own_parts(layer))
@@ -270,11 +270,11 @@
         y_order = x_order[::-1] if layer == layers - 1 else x_order
         for x_part, y_part in zip(x_order, y_order):
             arrive(own_x(kind, layer, x_peer, me, (x_part,)))
-            if x_part in ((0, 2), (2, 6)):
+            if x_part in ((0, 2), (0, 1)):
                 start(far(kind, layer, 0, x_peer, y_peer))
             start(pair(kind, layer, x_peer, "pair_x", (x_part,)))
             arrive(own_y(1 - kind, layer, y_peer, me, (y_part,)))
-            if y_part == (1, 2):
+            if y_part in ((1, 2), (0, 1)):
                 start(far(1 - kind, layer, 1, y_peer, x_peer))
             start(pair(1 - kind, layer, y_peer, "pair_y", (y_part,)))
 
@@ -316,11 +316,9 @@
         pack(kind, x_peer, p2)
         pack(1 - kind, y_peer, p4)
         near_partner(kind, 2)
-        far_arrive(kind, 2, 0)
         pack(kind, partner_of(x_peer), p3)
-        far_arrive(kind, 2, 1)
         pack(1 - kind, partner_of(y_peer), p5)
-        far_arrive(kind, 2, 2)
+        far_arrive(kind, 2)
         far_partner(kind, 2)
 
     by_kind(stage_own)

time: 63.9 us -> 64.8 us (1.014)
  Pallas kernels: 63.1 us -> 64 us
    pallas_call x1, Pallas kernels: 55.5 us -> 56.4 us  [local_step(): pl.pallas_call(functools.partial(gather_kernel, dims), name='gather_step'...]
where the time goes in v8:
time: 64.8 us; the launch traced here: 64.7 us
  Pallas kernels  64 us (99%)
  between operations  0.66 us (1%)
    pallas_call x1, Pallas kernels, local_step(): pl.pallas_call(functools.partial(gather_kernel, dims), name='gather_step'...  56.4 us
    pallas_call x1, Pallas kernels, local_step(): pl.pallas_call(functools.partial(finish_kernel, dims), name='finish', out...  7.65 us

profile of v8, /device:TPU:0, one launch (start us, length us, event | category | flops | bytes accessed | tf_op | source)
XLA Modules:
  0.0 64.7 jit_solution(7993567712716516006)
XLA Ops:
  0.6 0.0 copy-start
  0.6 56.4 %gather_step.1 = (bf16[6912,128]{1,0:T(8,128)(2,1)S(1)}, bf16[6912,128]{1,0:T(8,128)(2,1)S(1)}, bf16[6912,128]{1,0:T(8,128)(2,1)S(1)}, bf16[6912,128]{1,0:T(8,12...) custom-call(f32[1728,3,128]{2,1,0:T(4,128)} %bitcast.43, ...), custom_call_target="tpu_custom_call" | custom-call | tf_op jit(solution)/shard_map/gather_step/pallas_call | solution.py:422
  57.0 0.0 copy-done
  57.0 7.6 %finish.1 = (bf16[13824,3,128]{2,1,0:T(4,128)(2,1)}, f32[1728,3,128]{2,1,0:T(4,128)}, f32[1728,3,128]{2,1,0:T(4,128)}, f32[1728,3,128]{2,1,0:T(4,128)}, f32[4,128]{1,0:T(4,128)}) custom-call(bf16[1728,3,128]{2,1,0:T(4,128)(2,1)S(1)} %bitcast.37, bf16[1728,3,128]{2,1,0:T(4,128)(2,1)S(1)} %bitcast.38, bf16[1728,3,128]{2,1,0:T(4,128)(2,1)S(1)} %bitcast.39, ...), custom_call_target="tpu_custom_call" | custom-call | tf_op jit(solution)/shard_map/finish/pallas_call | solution.py:442
Async XLA Ops:
  0.6 56.4 %copy-start = (bf16[512,768]{1,0:T(8,128)(2,1)S(1)}, bf16[512,768]{1,0:T(8,128)(2,1)}, u32[]{:S(2)}) copy-start(bf16[512,768]{1,0:T(8,128)(2,1)} %tgt_ref.1) | copy-start | bytes 2359300

commit v9 on v7

--- a/solution.py
+++ b/solution.py
@@ -76,7 +76,7 @@
                   p0, p1, p2, p3, p4, p5, master_out, one_out, two_out, w_in, w_out, hidden_ref,
                   grad_v, master_v, one_v, two_v,
                   part_ref, wide_ref, normed_ref, active_ref,
-                  load_sem, part_send, part_recv, send_sem, recv_sem):
+                  load_sem, grad_sem, part_send, part_recv, send_sem, recv_sem):
     layers, model_dim, hidden_dim, rows, chunks = dims
     in_rows = chunks * LANES // hidden_dim
     out_rows = chunks * LANES // model_dim
@@ -90,8 +90,15 @@
         src, dst = state[which]
         return pltpu.make_async_copy(src.at[:, layer, :], dst.at[layer], load_sem.at[which, layer])
 
+    span = chunks // 3
+
+    def grad_load(layer, part):
+        at = pl.ds(part * span, span)
+        return pltpu.make_async_copy(grad_hbm.at[at, layer, :], grad_v.at[layer, at], grad_sem.at[layer, part])
+
     for layer in range(layers):
-        load(0, layer).start()
+        for part in range(3):
+            grad_load(layer, part).start()
     tok_load = pltpu.make_async_copy(tok_hbm, hidden_ref, load_sem.at[4, 0])
 
     barrier = pltpu.get_barrier_semaphore()
@@ -100,19 +107,20 @@
 
     sums = tuple(jnp.zeros((8, LANES), F32) for _ in range(8))
     for layer in range(layers):
-        load(0, layer).wait()
-        if layer == layers - 1:
-            for which in range(1, 4):
-                load(which, 0).start()
-
-        def square(idx, carry):
-            base = pl.multiple_of(idx * 64, 64)
-            block = grad_v[layer, pl.ds(base, 64), :]
-            return tuple(carry[k] + block[8 * k:8 * k + 8] * block[8 * k:8 * k + 8] for k in range(8))
-
-        sums = lax.fori_loop(0, chunks // 64, square, sums)
+        for part in range(3):
+            grad_load(layer, part).wait()
+            if layer == layers - 1 and part == 2:
+                for which in range(1, 4):
+                    load(which, 0).start()
+
+            def square(idx, carry):
+                base = pl.multiple_of(part * span + idx * 64, 64)
+                block = grad_v[layer, pl.ds(base, 64), :]
+                return tuple(carry[k] + block[8 * k:8 * k + 8] * block[8 * k:8 * k + 8] for k in range(8))
+
+            sums = lax.fori_loop(0, span // 64, square, sums)
     mine = ((sums[0] + sums[1]) + (sums[2] + sums[3])) + ((sums[4] + sums[5]) + (sums[6] + sums[7]))
-    part_ref[me] = mine
+    part_ref[me] = jnp.sum(mine, axis=0, keepdims=True)
     pl.semaphore_wait(barrier, GROUP - 1)
 
     def part_copy(step):
@@ -139,7 +147,7 @@
     total = part_ref[0]
     for slot in range(1, GROUP):
         total = total + part_ref[slot]
-    total = jnp.sum(jnp.sum(total, axis=0, keepdims=True), axis=1, keepdims=True)
+    total = jnp.sum(total, axis=1, keepdims=True)
     clip = jnp.minimum(1.0, CLIP_NORM / jnp.sqrt(total))
     clip = jnp.broadcast_to(clip, (8, LANES))
 
@@ -265,6 +273,26 @@
     def partner_of(device):
         return device + 1 - 2 * core
 
+    def drain(kind):
+        for layer in range(layers):
+            left(own_x(kind, layer, me, x_peer))
+            left(own_y(kind, layer, me, y_peer))
+            left(pair(kind, layer, me, "pair_own", own_parts(layer)))
+            left(pair(kind, layer, x_peer, "pair_x", own_parts(layer)))
+            left(pair(1 - kind, layer, y_peer, "pair_y", own_parts(layer)))
+            if layer < layers - 1:
+                left(pair(1 - kind, layer, diag, "pair_far", far_parts(layer, 0) + far_parts(layer, 1)))
+                left(far(kind, layer, 0, x_peer, y_peer))
+                left(far(1 - kind, layer, 1, y_peer, x_peer))
+        for step in range(1, GROUP):
+            part_copy(step).wait_send()
+
+    def drain_last(kind):
+        layer = layers - 1
+        left(far(kind, layer, 0, x_peer, y_peer))
+        left(far(1 - kind, layer, 1, y_peer, x_peer))
+        left(pair(1 - kind, layer, diag, "pair_far", far_parts(layer, 0) + far_parts(layer, 1)))
+
     def forward(kind, layer):
         x_order = own_parts(layer)
         y_order = x_order[::-1] if layer == layers - 1 else x_order
@@ -320,8 +348,10 @@
         pack(kind, partner_of(x_peer), p3)
         far_arrive(kind, 2, 1)
         pack(1 - kind, partner_of(y_peer), p5)
+        drain(kind)
         far_arrive(kind, 2, 2)
         far_partner(kind, 2)
+        drain_last(kind)
 
     by_kind(stage_own)
     tok_load.wait()
@@ -330,22 +360,6 @@
     mlp_block(dims, 1, w_in, w_out, hidden_ref, normed_ref, active_ref)
     by_kind(stage_two)
 
-    for step in range(1, GROUP):
-        part_copy(step).wait_send()
-
-    def drain(kind):
-        for layer in range(layers):
-            left(own_x(kind, layer, me, x_peer))
-            left(own_y(kind, layer, me, y_peer))
-            left(pair(kind, layer, me, "pair_own", own_parts(layer)))
-            left(pair(kind, layer, x_peer, "pair_x", own_parts(layer)))
-            left(pair(1 - kind, layer, y_peer, "pair_y", own_parts(layer)))
-            left(pair(1 - kind, layer, diag, "pair_far", far_parts(layer, 0) + far_parts(layer, 1)))
-            left(far(kind, layer, 0, x_peer, y_peer))
-            left(far(1 - kind, layer, 1, y_peer, x_peer))
-
-    by_kind(drain)
-
 
 def finish_kernel(dims, p0, p1, p2, p3, p4, p5, master_ref, one_ref, two_ref, w_in, w_out, last_ref, tgt_ref,
                   packed_hbm, master_hbm, one_hbm, two_hbm, loss_hbm,
@@ -355,11 +369,11 @@
     twin = 1 - 2 * core
 
     copies = []
-    for idx, (ref, device) in enumerate(((p0, me), (p1, me + twin), (p2, x_peer), (p3, x_peer + twin), (p4, y_peer), (p5, y_peer + twin))):
-        copies.append(pltpu.make_async_copy(ref, packed_hbm.at[pl.ds(device * chunks, chunks)], sem.at[idx]))
     for which, (src, dst) in enumerate(((master_ref, master_hbm), (one_ref, one_hbm), (two_ref, two_hbm))):
         for layer in range(layers):
             copies.append(pltpu.make_async_copy(src.at[layer], dst.at[:, layer, :], sem.at[6 + which * layers + layer]))
+    for idx, (ref, device) in enumerate(((p0, me), (p1, me + twin), (p2, x_peer), (p3, x_peer + twin), (p4, y_peer), (p5, y_peer + twin))):
+        copies.append(pltpu.make_async_copy(ref, packed_hbm.at[pl.ds(device * chunks, chunks)], sem.at[idx]))
     for item in copies:
         item.start()
 
@@ -429,9 +443,10 @@
             out_specs=(vmem,) * 12,
             scratch_shapes=[
                 state_v, state_v, state_v, state_v,
-                pltpu.VMEM((group_size, 8, LANES), F32),
+                pltpu.VMEM((group_size, 1, LANES), F32),
                 wide_v, normed_v, active_v,
                 pltpu.SemaphoreType.DMA((5, layers)),
+                pltpu.SemaphoreType.DMA((layers, 3)),
                 pltpu.SemaphoreType.DMA((group_size,)),
                 pltpu.SemaphoreType.DMA((group_size,)),
                 pltpu.SemaphoreType.DMA((96,)),

time: 63.9 us -> 63.5 us (level)
  no operation moved by 1% of the time
where the time goes in v9:
time: 63.5 us; the launch traced here: 63.4 us
  Pallas kernels  62.7 us (99%)
  between operations  0.66 us (1%)
    pallas_call x1, Pallas kernels, local_step(): pl.pallas_call(functools.partial(gather_kernel, dims), name='gather_step'...  55.1 us
    pallas_call x1, Pallas kernels, local_step(): pl.pallas_call(functools.partial(finish_kernel, dims), name='finish', out...  7.62 us

profile of v9, /device:TPU:0, one launch (start us, length us, event | category | flops | bytes accessed | tf_op | source)
XLA Modules:
  0.0 63.4 jit_solution(12516126886390476205)
XLA Ops:
  0.6 0.0 copy-start
  0.6 55.1 %gather_step.1 = (bf16[6912,128]{1,0:T(8,128)(2,1)S(1)}, bf16[6912,128]{1,0:T(8,128)(2,1)S(1)}, bf16[6912,128]{1,0:T(8,128)(2,1)S(1)}, bf16[6912,128]{1,0:T(8,12...) custom-call(f32[1728,3,128]{2,1,0:T(4,128)} %bitcast.43, ...), custom_call_target="tpu_custom_call" | custom-call | tf_op jit(solution)/shard_map/gather_step/pallas_call | solution.py:438
  55.8 0.0 copy-done
  55.8 7.6 %finish.1 = (bf16[13824,3,128]{2,1,0:T(4,128)(2,1)}, f32[1728,3,128]{2,1,0:T(4,128)}, f32[1728,3,128]{2,1,0:T(4,128)}, f32[1728,3,128]{2,1,0:T(4,128)}, f32[4,128]{1,0:T(4,128)}) custom-call(bf16[1728,3,128]{2,1,0:T(4,128)(2,1)S(1)} %bitcast.37, bf16[1728,3,128]{2,1,0:T(4,128)(2,1)S(1)} %bitcast.38, bf16[1728,3,128]{2,1,0:T(4,128)(2,1)S(1)} %bitcast.39, ...), custom_call_target="tpu_custom_call" | custom-call | tf_op jit(solution)/shard_map/finish/pallas_call | solution.py:459
Async XLA Ops:
  0.6 55.1 %copy-start = (bf16[512,768]{1,0:T(8,128)(2,1)S(1)}, bf16[512,768]{1,0:T(8,128)(2,1)}, u32[]{:S(2)}) copy-start(bf16[512,768]{1,0:T(8,128)(2,1)} %tgt_ref.1) | copy-start | bytes 2359300

commit v10 on v9

--- a/solution.py
+++ b/solution.py
@@ -90,14 +90,15 @@
         src, dst = state[which]
         return pltpu.make_async_copy(src.at[:, layer, :], dst.at[layer], load_sem.at[which, layer])
 
-    span = chunks // 3
+    loads = 9
+    span = chunks // loads
 
     def grad_load(layer, part):
         at = pl.ds(part * span, span)
         return pltpu.make_async_copy(grad_hbm.at[at, layer, :], grad_v.at[layer, at], grad_sem.at[layer, part])
 
     for layer in range(layers):
-        for part in range(3):
+        for part in range(loads):
             grad_load(layer, part).start()
     tok_load = pltpu.make_async_copy(tok_hbm, hidden_ref, load_sem.at[4, 0])
 
@@ -107,9 +108,9 @@
 
     sums = tuple(jnp.zeros((8, LANES), F32) for _ in range(8))
     for layer in range(layers):
-        for part in range(3):
+        for part in range(loads):
             grad_load(layer, part).wait()
-            if layer == layers - 1 and part == 2:
+            if layer == layers - 1 and part == loads - 1:
                 for which in range(1, 4):
                     load(which, 0).start()
 
@@ -157,7 +158,7 @@
         ref, count = ((w_in, in_rows), (w_out, out_rows))[kind]
         span = count // part[1]
         at = lax.rem(device, 4) * count + part[0] * span
-        return ref.at[layer, pl.ds(pl.multiple_of(at, 16), span), :]
+        return ref.at[layer, pl.ds(pl.multiple_of(at, 8), span), :]
 
     def copies(kind, layer, device, route, target, parts):
         out = []
@@ -185,7 +186,7 @@
         return ((0, 6), (1, 6), (2, 6), (1, 2)) if layer == 0 else ((0, 2), (1, 2))
 
     def far_parts(layer, half):
-        return tuple((3 * half + at, 6) for at in range(3)) if layer == layers - 1 else ((half, 2),)
+        return ((3 * half, 6), (3 * half + 1, 6), (6 * half + 4, 12), (6 * half + 5, 12)) if layer == layers - 1 else ((half, 2),)
 
     def own_x(kind, layer, device, target, parts=None):
         return copies(kind, layer, device, "own_x", target, parts or own_parts(layer))
@@ -350,6 +351,7 @@
         pack(1 - kind, partner_of(y_peer), p5)
         drain(kind)
         far_arrive(kind, 2, 2)
+        far_arrive(kind, 2, 3)
         far_partner(kind, 2)
         drain_last(kind)
 
@@ -446,7 +448,7 @@
                 pltpu.VMEM((group_size, 1, LANES), F32),
                 wide_v, normed_v, active_v,
                 pltpu.SemaphoreType.DMA((5, layers)),
-                pltpu.SemaphoreType.DMA((layers, 3)),
+                pltpu.SemaphoreType.DMA((layers, 9)),
                 pltpu.SemaphoreType.DMA((group_size,)),
                 pltpu.SemaphoreType.DMA((group_size,)),
                 pltpu.SemaphoreType.DMA((96,)),

time: 63.5 us -> 63.7 us (level)
  no operation moved by 1% of the time
where the time goes in v10:
time: 63.7 us; the launch traced here: 63.6 us
  Pallas kernels  62.9 us (99%)
  between operations  0.66 us (1%)
    pallas_call x1, Pallas kernels, local_step(): pl.pallas_call(functools.partial(gather_kernel, dims), name='gather_step'...  55.3 us
    pallas_call x1, Pallas kernels, local_step(): pl.pallas_call(functools.partial(finish_kernel, dims), name='finish', out...  7.62 us

profile of v10, /device:TPU:0, one launch (start us, length us, event | category | flops | bytes accessed | tf_op | source)
XLA Modules:
  0.0 63.6 jit_solution(715032920542213948)
XLA Ops:
  0.6 0.0 copy-start
  0.6 55.3 %gather_step.1 = (bf16[6912,128]{1,0:T(8,128)(2,1)S(1)}, bf16[6912,128]{1,0:T(8,128)(2,1)S(1)}, bf16[6912,128]{1,0:T(8,128)(2,1)S(1)}, bf16[6912,128]{1,0:T(8,12...) custom-call(f32[1728,3,128]{2,1,0:T(4,128)} %bitcast.43, ...), custom_call_target="tpu_custom_call" | custom-call | tf_op jit(solution)/shard_map/gather_step/pallas_call | solution.py:440
  56.0 0.0 copy-done
  56.0 7.6 %finish.1 = (bf16[13824,3,128]{2,1,0:T(4,128)(2,1)}, f32[1728,3,128]{2,1,0:T(4,128)}, f32[1728,3,128]{2,1,0:T(4,128)}, f32[1728,3,128]{2,1,0:T(4,128)}, f32[4,128]{1,0:T(4,128)}) custom-call(bf16[1728,3,128]{2,1,0:T(4,128)(2,1)S(1)} %bitcast.37, bf16[1728,3,128]{2,1,0:T(4,128)(2,1)S(1)} %bitcast.38, bf16[1728,3,128]{2,1,0:T(4,128)(2,1)S(1)} %bitcast.39, ...), custom_call_target="tpu_custom_call" | custom-call | tf_op jit(solution)/shard_map/finish/pallas_call | solution.py:461
Async XLA Ops:
  0.6 55.3 %copy-start = (bf16[512,768]{1,0:T(8,128)(2,1)S(1)}, bf16[512,768]{1,0:T(8,128)(2,1)}, u32[]{:S(2)}) copy-start(bf16[512,768]{1,0:T(8,128)(2,1)} %tgt_ref.1) | copy-start | bytes 2359300

commit v11 on v9

--- a/solution.py
+++ b/solution.py
@@ -369,11 +369,15 @@
     twin = 1 - 2 * core
 
     copies = []
+    span = chunks // 3
     for which, (src, dst) in enumerate(((master_ref, master_hbm), (one_ref, one_hbm), (two_ref, two_hbm))):
         for layer in range(layers):
-            copies.append(pltpu.make_async_copy(src.at[layer], dst.at[:, layer, :], sem.at[6 + which * layers + layer]))
+            for part in range(3):
+                at = pl.ds(part * span, span)
+                copies.append(pltpu.make_async_copy(src.at[layer, at], dst.at[at, layer, :], sem.at[len(copies)]))
     for idx, (ref, device) in enumerate(((p0, me), (p1, me + twin), (p2, x_peer), (p3, x_peer + twin), (p4, y_peer), (p5, y_peer + twin))):
-        copies.append(pltpu.make_async_copy(ref, packed_hbm.at[pl.ds(device * chunks, chunks)], sem.at[idx]))
+        for part in range(3):
+            copies.append(pltpu.make_async_copy(ref.at[pl.ds(part * span, span)], packed_hbm.at[pl.ds(device * chunks + part * span, span)], sem.at[len(copies)]))
     for item in copies:
         item.start()
 
@@ -390,8 +394,9 @@
             return 0
 
         lax.fori_loop(0, 4 * chunks // 128, squeeze, 0)
-        far_copies.append(pltpu.make_async_copy(far_ref.at[idx], packed_hbm.at[pl.ds(device * chunks, chunks)], far_sem.at[idx]))
-        far_copies[-1].start()
+        for part in range(3):
+            far_copies.append(pltpu.make_async_copy(far_ref.at[idx, pl.ds(part * span, span)], packed_hbm.at[pl.ds(device * chunks + part * span, span)], far_sem.at[3 * idx + part]))
+            far_copies[-1].start()
 
     hidden_ref[...] = last_ref[...]
     mlp_block(dims, layers - 1, w_in, w_out, hidden_ref, normed_ref, active_ref)
@@ -405,7 +410,7 @@
             folded = folded + error[:, col:col + LANES]
         loss_ref[idx:idx + 1, :] = jnp.sum(folded.T, axis=0, keepdims=True) * (1.0 / model_dim)
 
-    loss_copy = pltpu.make_async_copy(loss_ref, loss_hbm, far_sem.at[2])
+    loss_copy = pltpu.make_async_copy(loss_ref, loss_hbm, far_sem.at[6])
     loss_copy.start()
     for item in copies + far_copies + [loss_copy]:
         item.wait()
@@ -467,8 +472,8 @@
                 pltpu.VMEM((rows // LANES, LANES), F32),
                 pltpu.VMEM((2, chunks, layers, LANES), BF16),
                 wide_v, normed_v, active_v, hidden_v,
-                pltpu.SemaphoreType.DMA((6 + 3 * layers,)),
-                pltpu.SemaphoreType.DMA((3,)),
+                pltpu.SemaphoreType.DMA((18 + 9 * layers,)),
+                pltpu.SemaphoreType.DMA((7,)),
             ],
             compiler_params=pltpu.CompilerParams(vmem_limit_bytes=14 << 20),
         )(*gathered, tgt_rows)

time: 63.5 us -> 63.8 us (level)
  no operation moved by 1% of the time
where the time goes in v11:
time: 63.8 us; the launch traced here: 63.6 us
  Pallas kernels  63 us (99%)
  between operations  0.66 us (1%)
    pallas_call x1, Pallas kernels, local_step(): pl.pallas_call(functools.partial(gather_kernel, dims), name='gather_step'...  55.1 us
    pallas_call x1, Pallas kernels, local_step(): pl.pallas_call(functools.partial(finish_kernel, dims), name='finish', out...  7.88 us

profile of v11, /device:TPU:0, one launch (start us, length us, event | category | flops | bytes accessed | tf_op | source)
XLA Modules:
  0.0 63.6 jit_solution(8287883656651045681)
XLA Ops:
  0.6 0.0 copy-start
  0.6 55.1 %gather_step.1 = (bf16[6912,128]{1,0:T(8,128)(2,1)S(1)}, bf16[6912,128]{1,0:T(8,128)(2,1)S(1)}, bf16[6912,128]{1,0:T(8,128)(2,1)S(1)}, bf16[6912,128]{1,0:T(8,12...) custom-call(f32[1728,3,128]{2,1,0:T(4,128)} %bitcast.43, ...), custom_call_target="tpu_custom_call" | custom-call | tf_op jit(solution)/shard_map/gather_step/pallas_call | solution.py:443
  55.8 0.0 copy-done
  55.8 7.9 %finish.1 = (bf16[13824,3,128]{2,1,0:T(4,128)(2,1)}, f32[1728,3,128]{2,1,0:T(4,128)}, f32[1728,3,128]{2,1,0:T(4,128)}, f32[1728,3,128]{2,1,0:T(4,128)}, f32[4,128]{1,0:T(4,128)}) custom-call(bf16[1728,3,128]{2,1,0:T(4,128)(2,1)S(1)} %bitcast.37, bf16[1728,3,128]{2,1,0:T(4,128)(2,1)S(1)} %bitcast.38, bf16[1728,3,128]{2,1,0:T(4,128)(2,1)S(1)} %bitcast.39, ...), custom_call_target="tpu_custom_call" | custom-call | tf_op jit(solution)/shard_map/finish/pallas_call | solution.py:464
Async XLA Ops:
  0.6 55.1 %copy-start = (bf16[512,768]{1,0:T(8,128)(2,1)S(1)}, bf16[512,768]{1,0:T(8,128)(2,1)}, u32[]{:S(2)}) copy-start(bf16[512,768]{1,0:T(8,128)(2,1)} %tgt_ref.1) | copy-start | bytes 2359300

commit v12 on v9

--- a/solution.py
+++ b/solution.py
@@ -287,11 +287,21 @@
         for step in range(1, GROUP):
             part_copy(step).wait_send()
 
-    def drain_last(kind):
-        layer = layers - 1
-        left(far(kind, layer, 0, x_peer, y_peer))
-        left(far(1 - kind, layer, 1, y_peer, x_peer))
-        left(pair(1 - kind, layer, diag, "pair_far", far_parts(layer, 0) + far_parts(layer, 1)))
+    def last_parts(half):
+        return far_parts(layers - 1, half)[-1:]
+
+    def start_far(kind, layer, half, device, target):
+        if layer < layers - 1:
+            start(far(kind, layer, half, device, target))
+            return
+        start(far(kind, layer, half, device, target, far_parts(layer, half)[:-1]))
+
+        @pl.when(core == 1)
+        def _():
+            start(far(kind, layer, half, device, target, last_parts(half)))
+
+    def extra(kind, half, device, route, target):
+        return copies(kind, layers - 1, device, route, target, last_parts(half))
 
     def forward(kind, layer):
         x_order = own_parts(layer)
@@ -299,11 +309,11 @@
         for x_part, y_part in zip(x_order, y_order):
             arrive(own_x(kind, layer, x_peer, me, (x_part,)))
             if x_part in ((0, 2), (2, 6)):
-                start(far(kind, layer, 0, x_peer, y_peer))
+                start_far(kind, layer, 0, x_peer, y_peer)
             start(pair(kind, layer, x_peer, "pair_x", (x_part,)))
             arrive(own_y(1 - kind, layer, y_peer, me, (y_part,)))
             if y_part == (1, 2):
-                start(far(1 - kind, layer, 1, y_peer, x_peer))
+                start_far(1 - kind, layer, 1, y_peer, x_peer)
             start(pair(1 - kind, layer, y_peer, "pair_y", (y_part,)))
 
     def far_arrive(kind, layer, only=None):
@@ -317,9 +327,9 @@
     def far_partner(kind, layer):
         arrive(pair(1 - kind, layer, partner_of(diag), "pair_far", far_parts(layer, 0) + far_parts(layer, 1)))
 
-    def near_partner(kind, layer):
-        arrive(pair(kind, layer, partner_of(x_peer), "pair_x", own_parts(layer)))
-        arrive(pair(1 - kind, layer, partner_of(y_peer), "pair_y", own_parts(layer)))
+    def near_partner(kind, layer, x_parts=None, y_parts=None):
+        arrive(pair(kind, layer, partner_of(x_peer), "pair_x", x_parts or own_parts(layer)))
+        arrive(pair(1 - kind, layer, partner_of(y_peer), "pair_y", y_parts or own_parts(layer)))
 
     def stage_own(kind):
         pack(kind, me, p0)
@@ -340,18 +350,50 @@
         far_partner(kind, 1)
 
     def stage_two(kind):
-        forward(kind, 2)
+        last = layers - 1
+        early = far_parts(last, 0)[:-1] + far_parts(last, 1)[:-1]
+        late = last_parts(0) + last_parts(1)
+        forward(kind, last)
+        near_partner(kind, last, ((0, 2),), ((1, 2),))
+
+        @pl.when(core == 1)
+        def _():
+            start(extra(kind, 0, partner_of(x_peer), "extra", y_peer))
+            start(extra(1 - kind, 1, partner_of(y_peer), "extra", x_peer))
+
         pack(kind, x_peer, p2)
         pack(1 - kind, y_peer, p4)
-        near_partner(kind, 2)
-        far_arrive(kind, 2, 0)
+        near_partner(kind, last, ((1, 2),), ((0, 2),))
+        far_arrive(kind, last, 0)
         pack(kind, partner_of(x_peer), p3)
-        far_arrive(kind, 2, 1)
+        far_arrive(kind, last, 1)
         pack(1 - kind, partner_of(y_peer), p5)
         drain(kind)
-        far_arrive(kind, 2, 2)
-        far_partner(kind, 2)
-        drain_last(kind)
+        arrive(pair(1 - kind, last, partner_of(diag), "pair_far", early))
+
+        @pl.when(core == 1)
+        def _():
+            far_arrive(kind, last, 2)
+            for half in range(2):
+                arrive(extra(1 - kind, half, partner_of(diag), "extra", me))
+                start(extra(1 - kind, half, partner_of(diag), "pair_extra", partner))
+            left(pair(1 - kind, last, diag, "pair_far", late))
+            left(far(kind, last, 0, x_peer, y_peer, last_parts(0)))
+            left(far(1 - kind, last, 1, y_peer, x_peer, last_parts(1)))
+            left(extra(kind, 0, partner_of(x_peer), "extra", y_peer))
+            left(extra(1 - kind, 1, partner_of(y_peer), "extra", x_peer))
+            for half in range(2):
+                left(extra(1 - kind, half, partner_of(diag), "pair_extra", partner))
+
+        @pl.when(core == 0)
+        def _():
+            arrive(pair(1 - kind, last, partner_of(diag), "pair_far", late))
+            for half in range(2):
+                arrive(extra(1 - kind, half, diag, "pair_extra", me))
+
+        left(pair(1 - kind, last, diag, "pair_far", early))
+        left(far(kind, last, 0, x_peer, y_peer, far_parts(last, 0)[:-1]))
+        left(far(1 - kind, last, 1, y_peer, x_peer, far_parts(last, 1)[:-1]))
 
     by_kind(stage_own)
     tok_load.wait()

time: 63.5 us -> 64.1 us (level)
  Pallas kernels: 62.7 us -> 63.4 us
    pallas_call x1, Pallas kernels: 55.1 us -> 55.8 us  [local_step(): pl.pallas_call(functools.partial(gather_kernel, dims), name='gather_step'...]
where the time goes in v12:
time: 64.1 us; the launch traced here: 64 us
  Pallas kernels  63.4 us (99%)
  between operations  0.66 us (1%)
    pallas_call x1, Pallas kernels, local_step(): pl.pallas_call(functools.partial(gather_kernel, dims), name='gather_step'...  55.8 us
    pallas_call x1, Pallas kernels, local_step(): pl.pallas_call(functools.partial(finish_kernel, dims), name='finish', out...  7.62 us

profile of v12, /device:TPU:0, one launch (start us, length us, event | category | flops | bytes accessed | tf_op | source)
XLA Modules:
  0.0 64.0 jit_solution(13350329201223432747)
XLA Ops:
  0.6 0.0 copy-start
  0.6 55.8 %gather_step.1 = (bf16[6912,128]{1,0:T(8,128)(2,1)S(1)}, bf16[6912,128]{1,0:T(8,128)(2,1)S(1)}, bf16[6912,128]{1,0:T(8,128)(2,1)S(1)}, bf16[6912,128]{1,0:T(8,12...) custom-call(f32[1728,3,128]{2,1,0:T(4,128)} %bitcast.43, ...), custom_call_target="tpu_custom_call" | custom-call | tf_op jit(solution)/shard_map/gather_step/pallas_call | solution.py:480
  56.4 0.0 copy-done
  56.4 7.6 %finish.1 = (bf16[13824,3,128]{2,1,0:T(4,128)(2,1)}, f32[1728,3,128]{2,1,0:T(4,128)}, f32[1728,3,128]{2,1,0:T(4,128)}, f32[1728,3,128]{2,1,0:T(4,128)}, f32[4,128]{1,0:T(4,128)}) custom-call(bf16[1728,3,128]{2,1,0:T(4,128)(2,1)S(1)} %bitcast.37, bf16[1728,3,128]{2,1,0:T(4,128)(2,1)S(1)} %bitcast.38, bf16[1728,3,128]{2,1,0:T(4,128)(2,1)S(1)} %bitcast.39, ...), custom_call_target="tpu_custom_call" | custom-call | tf_op jit(solution)/shard_map/finish/pallas_call | solution.py:501
Async XLA Ops:
  0.6 55.8 %copy-start = (bf16[512,768]{1,0:T(8,128)(2,1)S(1)}, bf16[512,768]{1,0:T(8,128)(2,1)}, u32[]{:S(2)}) copy-start(bf16[512,768]{1,0:T(8,128)(2,1)} %tgt_ref.1) | copy-start | bytes 2359300

commit v13 on v12

--- a/solution.py
+++ b/solution.py
@@ -296,7 +296,7 @@
             return
         start(far(kind, layer, half, device, target, far_parts(layer, half)[:-1]))
 
-        @pl.when(core == 1)
+        @pl.when(core == 0)
         def _():
             start(far(kind, layer, half, device, target, last_parts(half)))
 
@@ -356,7 +356,7 @@
         forward(kind, last)
         near_partner(kind, last, ((0, 2),), ((1, 2),))
 
-        @pl.when(core == 1)
+        @pl.when(core == 0)
         def _():
             start(extra(kind, 0, partner_of(x_peer), "extra", y_peer))
             start(extra(1 - kind, 1, partner_of(y_peer), "extra", x_peer))
@@ -371,7 +371,7 @@
         drain(kind)
         arrive(pair(1 - kind, last, partner_of(diag), "pair_far", early))
 
-        @pl.when(core == 1)
+        @pl.when(core == 0)
         def _():
             far_arrive(kind, last, 2)
             for half in range(2):
@@ -385,7 +385,7 @@
             for half in range(2):
                 left(extra(1 - kind, half, partner_of(diag), "pair_extra", partner))
 
-        @pl.when(core == 0)
+        @pl.when(core == 1)
         def _():
             arrive(pair(1 - kind, last, partner_of(diag), "pair_far", late))
             for half in range(2):

time: 64.1 us -> 63.4 us (0.989)
  Pallas kernels: 63.4 us -> 62.7 us
    pallas_call x1, Pallas kernels: 55.8 us -> 55 us  [local_step(): pl.pallas_call(functools.partial(gather_kernel, dims), name='gather_step'...]
where the time goes in v13:
time: 63.4 us; the launch traced here: 63.3 us
  Pallas kernels  62.7 us (99%)
  between operations  0.66 us (1%)
    pallas_call x1, Pallas kernels, local_step(): pl.pallas_call(functools.partial(gather_kernel, dims), name='gather_step'...  55 us
    pallas_call x1, Pallas kernels, local_step(): pl.pallas_call(functools.partial(finish_kernel, dims), name='finish', out...  7.62 us

profile of v13, /device:TPU:0, one launch (start us, length us, event | category | flops | bytes accessed | tf_op | source)
XLA Modules:
  0.0 63.3 jit_solution(14651907900099131173)
XLA Ops:
  0.6 0.0 copy-start
  0.6 55.0 %gather_step.1 = (bf16[6912,128]{1,0:T(8,128)(2,1)S(1)}, bf16[6912,128]{1,0:T(8,128)(2,1)S(1)}, bf16[6912,128]{1,0:T(8,128)(2,1)S(1)}, bf16[6912,128]{1,0:T(8,12...) custom-call(f32[1728,3,128]{2,1,0:T(4,128)} %bitcast.43, ...), custom_call_target="tpu_custom_call" | custom-call | tf_op jit(solution)/shard_map/gather_step/pallas_call | solution.py:480
  55.7 0.0 copy-done
  55.7 7.6 %finish.1 = (bf16[13824,3,128]{2,1,0:T(4,128)(2,1)}, f32[1728,3,128]{2,1,0:T(4,128)}, f32[1728,3,128]{2,1,0:T(4,128)}, f32[1728,3,128]{2,1,0:T(4,128)}, f32[4,128]{1,0:T(4,128)}) custom-call(bf16[1728,3,128]{2,1,0:T(4,128)(2,1)S(1)} %bitcast.37, bf16[1728,3,128]{2,1,0:T(4,128)(2,1)S(1)} %bitcast.38, bf16[1728,3,128]{2,1,0:T(4,128)(2,1)S(1)} %bitcast.39, ...), custom_call_target="tpu_custom_call" | custom-call | tf_op jit(solution)/shard_map/finish/pallas_call | solution.py:501
Async XLA Ops:
  0.6 55.1 %copy-start = (bf16[512,768]{1,0:T(8,128)(2,1)S(1)}, bf16[512,768]{1,0:T(8,128)(2,1)}, u32[]{:S(2)}) copy-start(bf16[512,768]{1,0:T(8,128)(2,1)} %tgt_ref.1) | copy-start | bytes 2359300

commit v14 on v13

--- a/solution.py
+++ b/solution.py
@@ -157,7 +157,7 @@
         ref, count = ((w_in, in_rows), (w_out, out_rows))[kind]
         span = count // part[1]
         at = lax.rem(device, 4) * count + part[0] * span
-        return ref.at[layer, pl.ds(pl.multiple_of(at, 16), span), :]
+        return ref.at[layer, pl.ds(pl.multiple_of(at, 8), span), :]
 
     def copies(kind, layer, device, route, target, parts):
         out = []
@@ -185,7 +185,7 @@
         return ((0, 6), (1, 6), (2, 6), (1, 2)) if layer == 0 else ((0, 2), (1, 2))
 
     def far_parts(layer, half):
-        return tuple((3 * half + at, 6) for at in range(3)) if layer == layers - 1 else ((half, 2),)
+        return ((3 * half, 6), (3 * half + 1, 6), (6 * half + 4, 12), (6 * half + 5, 12)) if layer == layers - 1 else ((half, 2),)
 
     def own_x(kind, layer, device, target, parts=None):
         return copies(kind, layer, device, "own_x", target, parts or own_parts(layer))
@@ -369,11 +369,12 @@
         far_arrive(kind, last, 1)
         pack(1 - kind, partner_of(y_peer), p5)
         drain(kind)
+        far_arrive(kind, last, 2)
         arrive(pair(1 - kind, last, partner_of(diag), "pair_far", early))
 
         @pl.when(core == 0)
         def _():
-            far_arrive(kind, last, 2)
+            far_arrive(kind, last, 3)
             for half in range(2):
                 arrive(extra(1 - kind, half, partner_of(diag), "extra", me))
                 start(extra(1 - kind, half, partner_of(diag), "pair_extra", partner))

time: 63.4 us -> 63.6 us (level)
  no operation moved by 1% of the time
where the time goes in v14:
time: 63.6 us; the launch traced here: 63.4 us
  Pallas kernels  62.8 us (99%)
  between operations  0.66 us (1%)
    pallas_call x1, Pallas kernels, local_step(): pl.pallas_call(functools.partial(gather_kernel, dims), name='gather_step'...  55.2 us
    pallas_call x1, Pallas kernels, local_step(): pl.pallas_call(functools.partial(finish_kernel, dims), name='finish', out...  7.62 us

profile of v14, /device:TPU:0, one launch (start us, length us, event | category | flops | bytes accessed | tf_op | source)
XLA Modules:
  0.0 63.4 jit_solution(3528747782243398256)
XLA Ops:
  0.6 0.0 copy-start
  0.6 55.2 %gather_step.1 = (bf16[6912,128]{1,0:T(8,128)(2,1)S(1)}, bf16[6912,128]{1,0:T(8,128)(2,1)S(1)}, bf16[6912,128]{1,0:T(8,128)(2,1)S(1)}, bf16[6912,128]{1,0:T(8,12...) custom-call(f32[1728,3,128]{2,1,0:T(4,128)} %bitcast.43, ...), custom_call_target="tpu_custom_call" | custom-call | tf_op jit(solution)/shard_map/gather_step/pallas_call | solution.py:481
  55.8 0.0 copy-done
  55.8 7.6 %finish.1 = (bf16[13824,3,128]{2,1,0:T(4,128)(2,1)}, f32[1728,3,128]{2,1,0:T(4,128)}, f32[1728,3,128]{2,1,0:T(4,128)}, f32[1728,3,128]{2,1,0:T(4,128)}, f32[4,128]{1,0:T(4,128)}) custom-call(bf16[1728,3,128]{2,1,0:T(4,128)(2,1)S(1)} %bitcast.37, bf16[1728,3,128]{2,1,0:T(4,128)(2,1)S(1)} %bitcast.38, bf16[1728,3,128]{2,1,0:T(4,128)(2,1)S(1)} %bitcast.39, ...), custom_call_target="tpu_custom_call" | custom-call | tf_op jit(solution)/shard_map/finish/pallas_call | solution.py:502
Async XLA Ops:
  0.6 55.2 %copy-start = (bf16[512,768]{1,0:T(8,128)(2,1)S(1)}, bf16[512,768]{1,0:T(8,128)(2,1)}, u32[]{:S(2)}) copy-start(bf16[512,768]{1,0:T(8,128)(2,1)} %tgt_ref.1) | copy-start | bytes 2359300

commit v15 on v9

--- a/solution.py
+++ b/solution.py
@@ -73,7 +73,7 @@
 
 
 def gather_kernel(dims, grad_hbm, master_hbm, one_hbm, two_hbm, tok_hbm,
-                  p0, p1, p2, p3, p4, p5, master_out, one_out, two_out, w_in, w_out, hidden_ref,
+                  p0, p1, p2, p4, master_out, one_out, two_out, w_in, w_out, hidden_ref,
                   grad_v, master_v, one_v, two_v,
                   part_ref, wide_ref, normed_ref, active_ref,
                   load_sem, grad_sem, part_send, part_recv, send_sem, recv_sem):
@@ -345,9 +345,7 @@
         pack(1 - kind, y_peer, p4)
         near_partner(kind, 2)
         far_arrive(kind, 2, 0)
-        pack(kind, partner_of(x_peer), p3)
         far_arrive(kind, 2, 1)
-        pack(1 - kind, partner_of(y_peer), p5)
         drain(kind)
         far_arrive(kind, 2, 2)
         far_partner(kind, 2)
@@ -361,7 +359,7 @@
     by_kind(stage_two)
 
 
-def finish_kernel(dims, p0, p1, p2, p3, p4, p5, master_ref, one_ref, two_ref, w_in, w_out, last_ref, tgt_ref,
+def finish_kernel(dims, p0, p1, p2, p4, master_ref, one_ref, two_ref, w_in, w_out, last_ref, tgt_ref,
                   packed_hbm, master_hbm, one_hbm, two_hbm, loss_hbm,
                   loss_ref, far_ref, wide_ref, normed_ref, active_ref, hidden_ref, sem, far_sem):
     layers, model_dim, hidden_dim, rows, chunks = dims
@@ -372,17 +370,17 @@
     for which, (src, dst) in enumerate(((master_ref, master_hbm), (one_ref, one_hbm), (two_ref, two_hbm))):
         for layer in range(layers):
             copies.append(pltpu.make_async_copy(src.at[layer], dst.at[:, layer, :], sem.at[6 + which * layers + layer]))
-    for idx, (ref, device) in enumerate(((p0, me), (p1, me + twin), (p2, x_peer), (p3, x_peer + twin), (p4, y_peer), (p5, y_peer + twin))):
+    for idx, (ref, device) in enumerate(((p0, me), (p1, me + twin), (p2, x_peer), (p4, y_peer))):
         copies.append(pltpu.make_async_copy(ref, packed_hbm.at[pl.ds(device * chunks, chunks)], sem.at[idx]))
     for item in copies:
         item.start()
 
     far_copies = []
-    for idx, device in enumerate((diag, diag + twin)):
+    for idx, (device, flip) in enumerate(((x_peer + twin, 0), (y_peer + twin, 1), (diag, 1), (diag + twin, 1))):
         for y_value in range(2):
             @pl.when(y_pos == y_value)
             def _():
-                spread_piece(dims, 1 - y_value, device, (w_in, w_out), wide_ref)
+                spread_piece(dims, (y_value + flip) % 2, device, (w_in, w_out), wide_ref)
 
         def squeeze(at, _):
             block = wide_ref[pl.ds(pl.multiple_of(at * 128, 128), 128), :].astype(BF16).reshape(32, 4, LANES)
@@ -405,7 +403,7 @@
             folded = folded + error[:, col:col + LANES]
         loss_ref[idx:idx + 1, :] = jnp.sum(folded.T, axis=0, keepdims=True) * (1.0 / model_dim)
 
-    loss_copy = pltpu.make_async_copy(loss_ref, loss_hbm, far_sem.at[2])
+    loss_copy = pltpu.make_async_copy(loss_ref, loss_hbm, far_sem.at[4])
     loss_copy.start()
     for item in copies + far_copies + [loss_copy]:
         item.wait()
@@ -438,9 +436,9 @@
         gathered = pl.pallas_call(
             functools.partial(gather_kernel, dims),
             name="gather_step",
-            out_shape=(*(packed_v,) * 6, state_v, state_v, state_v, w_in_v, w_out_v, hidden_v),
+            out_shape=(*(packed_v,) * 4, state_v, state_v, state_v, w_in_v, w_out_v, hidden_v),
             in_specs=[hbm] * 5,
-            out_specs=(vmem,) * 12,
+            out_specs=(vmem,) * 10,
             scratch_shapes=[
                 state_v, state_v, state_v, state_v,
                 pltpu.VMEM((group_size, 1, LANES), F32),
@@ -454,23 +452,23 @@
             ],
             compiler_params=pltpu.CompilerParams(collective_id=0, has_side_effects=True, vmem_limit_bytes=19 << 20),
         )(*[pltpu.with_memory_space_constraint(a, pltpu.HBM) for a in (*tiled, tok_rows)])
-        gathered = [a.reshape(chunks, 4, LANES)[:, :layers, :] for a in gathered[:6]] + list(gathered[6:])
+        gathered = [a.reshape(chunks, 4, LANES)[:, :layers, :] for a in gathered[:4]] + list(gathered[4:])
         state_tile = jax.ShapeDtypeStruct((chunks, layers, LANES), F32)
         weights, new_master, new_one, new_two, row_loss = pl.pallas_call(
             functools.partial(finish_kernel, dims),
             name="finish",
             out_shape=(jax.ShapeDtypeStruct((chunks * group_size, layers, LANES), BF16), state_tile, state_tile, state_tile,
                        jax.ShapeDtypeStruct((rows // LANES, LANES), F32)),
-            in_specs=[vmem] * 13,
+            in_specs=[vmem] * 11,
             out_specs=(hbm,) * 5,
             scratch_shapes=[
                 pltpu.VMEM((rows // LANES, LANES), F32),
-                pltpu.VMEM((2, chunks, layers, LANES), BF16),
+                pltpu.VMEM((4, chunks, layers, LANES), BF16),
                 wide_v, normed_v, active_v, hidden_v,
                 pltpu.SemaphoreType.DMA((6 + 3 * layers,)),
-                pltpu.SemaphoreType.DMA((3,)),
+                pltpu.SemaphoreType.DMA((5,)),
             ],
-            compiler_params=pltpu.CompilerParams(vmem_limit_bytes=14 << 20),
+            compiler_params=pltpu.CompilerParams(vmem_limit_bytes=18 << 20),
         )(*gathered, tgt_rows)
 
         def flat(a):

time: 63.5 us -> 65.6 us (1.033)
  Pallas kernels: 62.7 us -> 64.8 us
    pallas_call x1, Pallas kernels: 7.62 us -> 9.8 us  [local_step(): pl.pallas_call(functools.partial(finish_kernel, dims), name='finish', out...]
where the time goes in v15:
time: 65.6 us; the launch traced here: 65.5 us
  Pallas kernels  64.8 us (99%)
  between operations  0.66 us (1%)
    pallas_call x1, Pallas kernels, local_step(): pl.pallas_call(functools.partial(gather_kernel, dims), name='gather_step'...  55 us
    pallas_call x1, Pallas kernels, local_step(): pl.pallas_call(functools.partial(finish_kernel, dims), name='finish', out...  9.8 us

profile of v15, /device:TPU:0, one launch (start us, length us, event | category | flops | bytes accessed | tf_op | source)
XLA Modules:
  0.0 65.5 jit_solution(14883603237089749965)
XLA Ops:
  0.6 0.0 copy-start
  0.6 55.0 %gather_step.1 = (bf16[6912,128]{1,0:T(8,128)(2,1)S(1)}, bf16[6912,128]{1,0:T(8,128)(2,1)S(1)}, bf16[6912,128]{1,0:T(8,128)(2,1)S(1)}, bf16[6912,128]{1,0:T(8,12...) custom-call(f32[1728,3,128]{2,1,0:T(4,128)} %bitcast.37, ...), custom_call_target="tpu_custom_call" | custom-call | tf_op jit(solution)/shard_map/gather_step/pallas_call | solution.py:436
  55.7 0.0 copy-done
  55.7 9.8 %finish.1 = (bf16[13824,3,128]{2,1,0:T(4,128)(2,1)}, f32[1728,3,128]{2,1,0:T(4,128)}, f32[1728,3,128]{2,1,0:T(4,128)}, f32[1728,3,128]{2,1,0:T(4,128)}, f32[4,128]{1,0:T(4,128)}) custom-call(bf16[1728,3,128]{2,1,0:T(4,128)(2,1)S(1)} %bitcast.33, bf16[1728,3,128]{2,1,0:T(4,128)(2,1)S(1)} %bitcast.34, bf16[1728,3,128]{2,1,0:T(4,128)(2,1)S(1)} %bitcast.35, ...), custom_call_target="tpu_custom_call" | custom-call | tf_op jit(solution)/shard_map/finish/pallas_call | solution.py:457
Async XLA Ops:
  0.6 55.1 %copy-start = (bf16[512,768]{1,0:T(8,128)(2,1)S(1)}, bf16[512,768]{1,0:T(8,128)(2,1)}, u32[]{:S(2)}) copy-start(bf16[512,768]{1,0:T(8,128)(2,1)} %tgt_ref.1) | copy-start | bytes 2359300

commit v16 on v9

--- a/solution.py
+++ b/solution.py
@@ -289,9 +289,38 @@
 
     def drain_last(kind):
         layer = layers - 1
-        left(far(kind, layer, 0, x_peer, y_peer))
-        left(far(1 - kind, layer, 1, y_peer, x_peer))
+        left(far(kind, layer, 0, x_peer, y_peer, far_parts(layer, 0)[:-1]))
+        left(far(1 - kind, layer, 1, y_peer, x_peer, far_parts(layer, 1)[:-1]))
+
+        @pl.when(chip != 0)
+        def _():
+            left(far(kind, layer, 0, x_peer, y_peer, far_parts(layer, 0)[-1:]))
+            left(far(1 - kind, layer, 1, y_peer, x_peer, far_parts(layer, 1)[-1:]))
+
+        @pl.when(chip == last_chip)
+        def _():
+            left(moved(kind, 0))
+            left(moved(kind, 1))
+
         left(pair(1 - kind, layer, diag, "pair_far", far_parts(layer, 0) + far_parts(layer, 1)))
+
+    chip = me // 2
+    last_chip = GROUP // 2 - 1
+
+    def start_far(kind, layer, half, device, target):
+        if layer < layers - 1:
+            start(far(kind, layer, half, device, target))
+            return
+        start(far(kind, layer, half, device, target, far_parts(layer, half)[:-1]))
+
+        @pl.when(chip != 0)
+        def _():
+            start(far(kind, layer, half, device, target, far_parts(layer, half)[-1:]))
+
+    def moved(kind, half):
+        source = (y_peer, x_peer)[half]
+        target = (x_peer, y_peer)[half]
+        return far((1 - kind, kind)[half], layers - 1, half, source, target, far_parts(layers - 1, half)[-1:])
 
     def forward(kind, layer):
         x_order = own_parts(layer)
@@ -299,11 +328,11 @@
         for x_part, y_part in zip(x_order, y_order):
             arrive(own_x(kind, layer, x_peer, me, (x_part,)))
             if x_part in ((0, 2), (2, 6)):
-                start(far(kind, layer, 0, x_peer, y_peer))
+                start_far(kind, layer, 0, x_peer, y_peer)
             start(pair(kind, layer, x_peer, "pair_x", (x_part,)))
             arrive(own_y(1 - kind, layer, y_peer, me, (y_part,)))
             if y_part == (1, 2):
-                start(far(1 - kind, layer, 1, y_peer, x_peer))
+                start_far(1 - kind, layer, 1, y_peer, x_peer)
             start(pair(1 - kind, layer, y_peer, "pair_y", (y_part,)))
 
     def far_arrive(kind, layer, only=None):
@@ -341,6 +370,12 @@
 
     def stage_two(kind):
         forward(kind, 2)
+
+        @pl.when(chip == last_chip)
+        def _():
+            start(moved(kind, 0))
+            start(moved(kind, 1))
+
         pack(kind, x_peer, p2)
         pack(1 - kind, y_peer, p4)
         near_partner(kind, 2)

time: 63.5 us -> 63.5 us (level)
  no operation moved by 1% of the time
where the time goes in v16:
time: 63.5 us; the launch traced here: 63.4 us
  Pallas kernels  62.7 us (99%)
  between operations  0.66 us (1%)
    pallas_call x1, Pallas kernels, local_step(): pl.pallas_call(functools.partial(gather_kernel, dims), name='gather_step'...  55.1 us
    pallas_call x1, Pallas kernels, local_step(): pl.pallas_call(functools.partial(finish_kernel, dims), name='finish', out...  7.62 us

profile of v16, /device:TPU:0, one launch (start us, length us, event | category | flops | bytes accessed | tf_op | source)
XLA Modules:
  0.0 63.4 jit_solution(9620510188285280707)
XLA Ops:
  0.6 0.0 copy-start
  0.6 55.1 %gather_step.1 = (bf16[6912,128]{1,0:T(8,128)(2,1)S(1)}, bf16[6912,128]{1,0:T(8,128)(2,1)S(1)}, bf16[6912,128]{1,0:T(8,128)(2,1)S(1)}, bf16[6912,128]{1,0:T(8,12...) custom-call(f32[1728,3,128]{2,1,0:T(4,128)} %bitcast.43, ...), custom_call_target="tpu_custom_call" | custom-call | tf_op jit(solution)/shard_map/gather_step/pallas_call | solution.py:473
  55.8 0.0 copy-done
  55.8 7.6 %finish.1 = (bf16[13824,3,128]{2,1,0:T(4,128)(2,1)}, f32[1728,3,128]{2,1,0:T(4,128)}, f32[1728,3,128]{2,1,0:T(4,128)}, f32[1728,3,128]{2,1,0:T(4,128)}, f32[4,128]{1,0:T(4,128)}) custom-call(bf16[1728,3,128]{2,1,0:T(4,128)(2,1)S(1)} %bitcast.37, bf16[1728,3,128]{2,1,0:T(4,128)(2,1)S(1)} %bitcast.38, bf16[1728,3,128]{2,1,0:T(4,128)(2,1)S(1)} %bitcast.39, ...), custom_call_target="tpu_custom_call" | custom-call | tf_op jit(solution)/shard_map/finish/pallas_call | solution.py:494
Async XLA Ops:
  0.6 55.1 %copy-start = (bf16[512,768]{1,0:T(8,128)(2,1)S(1)}, bf16[512,768]{1,0:T(8,128)(2,1)}, u32[]{:S(2)}) copy-start(bf16[512,768]{1,0:T(8,128)(2,1)} %tgt_ref.1) | copy-start | bytes 2359300

commit v17 on v9

--- a/solution.py
+++ b/solution.py
@@ -74,7 +74,7 @@
 
 def gather_kernel(dims, grad_hbm, master_hbm, one_hbm, two_hbm, tok_hbm,
                   p0, p1, p2, p3, p4, p5, master_out, one_out, two_out, w_in, w_out, hidden_ref,
-                  grad_v, master_v, one_v, two_v,
+                  grad_t, grad_v, master_v, one_v, two_v,
                   part_ref, wide_ref, normed_ref, active_ref,
                   load_sem, grad_sem, part_send, part_recv, send_sem, recv_sem):
     layers, model_dim, hidden_dim, rows, chunks = dims
@@ -92,33 +92,35 @@
 
     span = chunks // 3
 
-    def grad_load(layer, part):
+    loads = 9
+    span = chunks // loads
+
+    def grad_load(part):
         at = pl.ds(part * span, span)
-        return pltpu.make_async_copy(grad_hbm.at[at, layer, :], grad_v.at[layer, at], grad_sem.at[layer, part])
-
-    for layer in range(layers):
-        for part in range(3):
-            grad_load(layer, part).start()
+        return pltpu.make_async_copy(grad_hbm.at[at], grad_t.at[at], grad_sem.at[part])
+
+    for part in range(loads):
+        grad_load(part).start()
     tok_load = pltpu.make_async_copy(tok_hbm, hidden_ref, load_sem.at[4, 0])
 
     barrier = pltpu.get_barrier_semaphore()
     for step in range(1, GROUP):
         pl.semaphore_signal(barrier, inc=1, device_id=(lax.rem(me + step, GROUP),), device_id_type=MESH)
 
-    sums = tuple(jnp.zeros((8, LANES), F32) for _ in range(8))
-    for layer in range(layers):
-        for part in range(3):
-            grad_load(layer, part).wait()
-            if layer == layers - 1 and part == 2:
-                for which in range(1, 4):
-                    load(which, 0).start()
-
-            def square(idx, carry):
-                base = pl.multiple_of(part * span + idx * 64, 64)
-                block = grad_v[layer, pl.ds(base, 64), :]
-                return tuple(carry[k] + block[8 * k:8 * k + 8] * block[8 * k:8 * k + 8] for k in range(8))
-
-            sums = lax.fori_loop(0, span // 64, square, sums)
+    sums = tuple(jnp.zeros((layers, LANES), F32) for _ in range(8))
+    for part in range(loads):
+        grad_load(part).wait()
+        if part == loads - 1:
+            for which in range(4):
+                load(which, 0).start()
+
+        def square(idx, carry):
+            block = grad_t[pl.ds(part * span + idx * 16, 16), :, :]
+            for k in range(16):
+                carry = carry[:k % 8] + (carry[k % 8] + block[k] * block[k],) + carry[k % 8 + 1:]
+            return carry
+
+        sums = lax.fori_loop(0, span // 16, square, sums)
     mine = ((sums[0] + sums[1]) + (sums[2] + sums[3])) + ((sums[4] + sums[5]) + (sums[6] + sums[7]))
     part_ref[me] = jnp.sum(mine, axis=0, keepdims=True)
     pl.semaphore_wait(barrier, GROUP - 1)
@@ -139,7 +141,7 @@
     for step in range(1, GROUP):
         part_copy(step).start()
     for item in range(1, layers):
-        for which in range(1, 4):
+        for which in range(4):
             load(which, item).start()
     tok_load.start()
     for step in range(1, GROUP):
@@ -246,7 +248,7 @@
         lax.fori_loop(0, count // 16 // part[1], body, 0)
 
     for layer in range(layers):
-        for which in range(1, 4):
+        for which in range(4):
             load(which, layer).wait()
         for part in own_parts(layer):
             adam(layer, part)
@@ -442,17 +444,18 @@
             in_specs=[hbm] * 5,
             out_specs=(vmem,) * 12,
             scratch_shapes=[
+                pltpu.VMEM((chunks, layers, LANES), F32),
                 state_v, state_v, state_v, state_v,
                 pltpu.VMEM((group_size, 1, LANES), F32),
                 wide_v, normed_v, active_v,
                 pltpu.SemaphoreType.DMA((5, layers)),
-                pltpu.SemaphoreType.DMA((layers, 3)),
+                pltpu.SemaphoreType.DMA((9,)),
                 pltpu.SemaphoreType.DMA((group_size,)),
                 pltpu.SemaphoreType.DMA((group_size,)),
                 pltpu.SemaphoreType.DMA((96,)),
                 pltpu.SemaphoreType.DMA((96,)),
             ],
-            compiler_params=pltpu.CompilerParams(collective_id=0, has_side_effects=True, vmem_limit_bytes=19 << 20),
+            compiler_params=pltpu.CompilerParams(collective_id=0, has_side_effects=True, vmem_limit_bytes=23 << 20),
         )(*[pltpu.with_memory_space_constraint(a, pltpu.HBM) for a in (*tiled, tok_rows)])
         gathered = [a.reshape(chunks, 4, LANES)[:, :layers, :] for a in gathered[:6]] + list(gathered[6:])
         state_tile = jax.ShapeDtypeStruct((chunks, layers, LANES), F32)

time: 63.5 us -> 63.6 us (level)
  no operation moved by 1% of the time
where the time goes in v17:
time: 63.6 us; the launch traced here: 63.5 us
  Pallas kernels  62.8 us (99%)
  between operations  0.66 us (1%)
    pallas_call x1, Pallas kernels, local_step(): pl.pallas_call(functools.partial(gather_kernel, dims), name='gather_step'...  55.2 us
    pallas_call x1, Pallas kernels, local_step(): pl.pallas_call(functools.partial(finish_kernel, dims), name='finish', out...  7.62 us

profile of v17, /device:TPU:0, one launch (start us, length us, event | category | flops | bytes accessed | tf_op | source)
XLA Modules:
  0.0 63.5 jit_solution(5670184669253237707)
XLA Ops:
  0.6 0.0 copy-start
  0.6 55.2 %gather_step.1 = (bf16[6912,128]{1,0:T(8,128)(2,1)S(1)}, bf16[6912,128]{1,0:T(8,128)(2,1)S(1)}, bf16[6912,128]{1,0:T(8,128)(2,1)S(1)}, bf16[6912,128]{1,0:T(8,12...) custom-call(f32[1728,3,128]{2,1,0:T(4,128)} %bitcast.43, ...), custom_call_target="tpu_custom_call" | custom-call | tf_op jit(solution)/shard_map/gather_step/pallas_call | solution.py:440
  55.9 0.0 copy-done
  55.9 7.6 %finish.1 = (bf16[13824,3,128]{2,1,0:T(4,128)(2,1)}, f32[1728,3,128]{2,1,0:T(4,128)}, f32[1728,3,128]{2,1,0:T(4,128)}, f32[1728,3,128]{2,1,0:T(4,128)}, f32[4,128]{1,0:T(4,128)}) custom-call(bf16[1728,3,128]{2,1,0:T(4,128)(2,1)S(1)} %bitcast.37, bf16[1728,3,128]{2,1,0:T(4,128)(2,1)S(1)} %bitcast.38, bf16[1728,3,128]{2,1,0:T(4,128)(2,1)S(1)} %bitcast.39, ...), custom_call_target="tpu_custom_call" | custom-call | tf_op jit(solution)/shard_map/finish/pallas_call | solution.py:462
Async XLA Ops:
  0.6 55.2 %copy-start = (bf16[512,768]{1,0:T(8,128)(2,1)S(1)}, bf16[512,768]{1,0:T(8,128)(2,1)}, u32[]{:S(2)}) copy-start(bf16[512,768]{1,0:T(8,128)(2,1)} %tgt_ref.1) | copy-start | bytes 2359300

commit v18 on v9

--- a/solution.py
+++ b/solution.py
@@ -157,7 +157,7 @@
         ref, count = ((w_in, in_rows), (w_out, out_rows))[kind]
         span = count // part[1]
         at = lax.rem(device, 4) * count + part[0] * span
-        return ref.at[layer, pl.ds(pl.multiple_of(at, 16), span), :]
+        return ref.at[layer, pl.ds(pl.multiple_of(at, 8), span), :]
 
     def copies(kind, layer, device, route, target, parts):
         out = []
@@ -185,7 +185,7 @@
         return ((0, 6), (1, 6), (2, 6), (1, 2)) if layer == 0 else ((0, 2), (1, 2))
 
     def far_parts(layer, half):
-        return tuple((3 * half + at, 6) for at in range(3)) if layer == layers - 1 else ((half, 2),)
+        return ((3 * half, 6), (3 * half + 1, 6), (6 * half + 4, 12), (6 * half + 5, 12)) if layer == layers - 1 else ((half, 2),)
 
     def own_x(kind, layer, device, target, parts=None):
         return copies(kind, layer, device, "own_x", target, parts or own_parts(layer))
@@ -350,6 +350,7 @@
         pack(1 - kind, partner_of(y_peer), p5)
         drain(kind)
         far_arrive(kind, 2, 2)
+        far_arrive(kind, 2, 3)
         far_partner(kind, 2)
         drain_last(kind)
 

time: 63.5 us -> 63.5 us (level)
  no operation moved by 1% of the time
where the time goes in v18:
time: 63.5 us; the launch traced here: 63.4 us
  Pallas kernels  62.7 us (99%)
  between operations  0.66 us (1%)
    pallas_call x1, Pallas kernels, local_step(): pl.pallas_call(functools.partial(gather_kernel, dims), name='gather_step'...  55.1 us
    pallas_call x1, Pallas kernels, local_step(): pl.pallas_call(functools.partial(finish_kernel, dims), name='finish', out...  7.62 us

profile of v18, /device:TPU:0, one launch (start us, length us, event | category | flops | bytes accessed | tf_op | source)
XLA Modules:
  0.0 63.4 jit_solution(6397511244715608600)
XLA Ops:
  0.6 0.0 copy-start
  0.6 55.1 %gather_step.1 = (bf16[6912,128]{1,0:T(8,128)(2,1)S(1)}, bf16[6912,128]{1,0:T(8,128)(2,1)S(1)}, bf16[6912,128]{1,0:T(8,128)(2,1)S(1)}, bf16[6912,128]{1,0:T(8,12...) custom-call(f32[1728,3,128]{2,1,0:T(4,128)} %bitcast.43, ...), custom_call_target="tpu_custom_call" | custom-call | tf_op jit(solution)/shard_map/gather_step/pallas_call | solution.py:439
  55.8 0.0 copy-done
  55.8 7.6 %finish.1 = (bf16[13824,3,128]{2,1,0:T(4,128)(2,1)}, f32[1728,3,128]{2,1,0:T(4,128)}, f32[1728,3,128]{2,1,0:T(4,128)}, f32[1728,3,128]{2,1,0:T(4,128)}, f32[4,128]{1,0:T(4,128)}) custom-call(bf16[1728,3,128]{2,1,0:T(4,128)(2,1)S(1)} %bitcast.37, bf16[1728,3,128]{2,1,0:T(4,128)(2,1)S(1)} %bitcast.38, bf16[1728,3,128]{2,1,0:T(4,128)(2,1)S(1)} %bitcast.39, ...), custom_call_target="tpu_custom_call" | custom-call | tf_op jit(solution)/shard_map/finish/pallas_call | solution.py:460
Async XLA Ops:
  0.6 55.1 %copy-start = (bf16[512,768]{1,0:T(8,128)(2,1)S(1)}, bf16[512,768]{1,0:T(8,128)(2,1)}, u32[]{:S(2)}) copy-start(bf16[512,768]{1,0:T(8,128)(2,1)} %tgt_ref.1) | copy-start | bytes 2359300

commit v19 on v13

--- a/solution.py
+++ b/solution.py
@@ -157,7 +157,7 @@
         ref, count = ((w_in, in_rows), (w_out, out_rows))[kind]
         span = count // part[1]
         at = lax.rem(device, 4) * count + part[0] * span
-        return ref.at[layer, pl.ds(pl.multiple_of(at, 16), span), :]
+        return ref.at[layer, pl.ds(pl.multiple_of(at, 8), span), :]
 
     def copies(kind, layer, device, route, target, parts):
         out = []
@@ -182,7 +182,7 @@
             item.wait_send()
 
     def own_parts(layer):
-        return ((0, 6), (1, 6), (2, 6), (1, 2)) if layer == 0 else ((0, 2), (1, 2))
+        return ((0, 12), (1, 12), (1, 6), (2, 6), (1, 2)) if layer == 0 else ((0, 2), (1, 2))
 
     def far_parts(layer, half):
         return tuple((3 * half + at, 6) for at in range(3)) if layer == layers - 1 else ((half, 2),)
@@ -234,16 +234,20 @@
         dst = w_in if kind == 0 else w_out
         slot = lax.rem(me, 4)
 
+        step = 16 if count // part[1] % 16 == 0 else 8
+
         def body(idx, _):
-            base = part[0] * (chunks // part[1]) + idx * (16 * per_row)
-            row = pl.multiple_of(slot * count + part[0] * (count // part[1]) + idx * 16, 16)
+            base = part[0] * (chunks // part[1]) + idx * (step * per_row)
+            row = pl.multiple_of(slot * count + part[0] * (count // part[1]) + idx * step, 8)
             for col in range(per_row):
-                top = master_out[layer, pl.ds(base + col, 8, stride=per_row), :]
-                low = master_out[layer, pl.ds(base + 8 * per_row + col, 8, stride=per_row), :]
-                dst[layer, pl.ds(row, 16), col * LANES:(col + 1) * LANES] = jnp.concatenate([top, low], axis=0).astype(BF16)
+                block = master_out[layer, pl.ds(base + col, 8, stride=per_row), :]
+                if step == 16:
+                    low = master_out[layer, pl.ds(base + 8 * per_row + col, 8, stride=per_row), :]
+                    block = jnp.concatenate([block, low], axis=0)
+                dst[layer, pl.ds(row, step), col * LANES:(col + 1) * LANES] = block.astype(BF16)
             return 0
 
-        lax.fori_loop(0, count // 16 // part[1], body, 0)
+        lax.fori_loop(0, count // step // part[1], body, 0)
 
     for layer in range(layers):
         for which in range(1, 4):

time: 63.4 us -> 63.3 us (level)
  no operation moved by 1% of the time
where the time goes in v19:
time: 63.3 us; the launch traced here: 63.2 us
  Pallas kernels  62.6 us (99%)
  between operations  0.66 us (1%)
    pallas_call x1, Pallas kernels, local_step(): pl.pallas_call(functools.partial(gather_kernel, dims), name='gather_step'...  54.9 us
    pallas_call x1, Pallas kernels, local_step(): pl.pallas_call(functools.partial(finish_kernel, dims), name='finish', out...  7.62 us

profile of v19, /device:TPU:0, one launch (start us, length us, event | category | flops | bytes accessed | tf_op | source)
XLA Modules:
  0.0 63.2 jit_solution(14704926840742336667)
XLA Ops:
  0.6 0.0 copy-start
  0.6 54.9 %gather_step.1 = (bf16[6912,128]{1,0:T(8,128)(2,1)S(1)}, bf16[6912,128]{1,0:T(8,128)(2,1)S(1)}, bf16[6912,128]{1,0:T(8,128)(2,1)S(1)}, bf16[6912,128]{1,0:T(8,12...) custom-call(f32[1728,3,128]{2,1,0:T(4,128)} %bitcast.43, ...), custom_call_target="tpu_custom_call" | custom-call | tf_op jit(solution)/shard_map/gather_step/pallas_call | solution.py:484
  55.6 0.0 copy-done
  55.6 7.6 %finish.1 = (bf16[13824,3,128]{2,1,0:T(4,128)(2,1)}, f32[1728,3,128]{2,1,0:T(4,128)}, f32[1728,3,128]{2,1,0:T(4,128)}, f32[1728,3,128]{2,1,0:T(4,128)}, f32[4,128]{1,0:T(4,128)}) custom-call(bf16[1728,3,128]{2,1,0:T(4,128)(2,1)S(1)} %bitcast.37, bf16[1728,3,128]{2,1,0:T(4,128)(2,1)S(1)} %bitcast.38, bf16[1728,3,128]{2,1,0:T(4,128)(2,1)S(1)} %bitcast.39, ...), custom_call_target="tpu_custom_call" | custom-call | tf_op jit(solution)/shard_map/finish/pallas_call | solution.py:505
Async XLA Ops:
  0.6 55.0 %copy-start = (bf16[512,768]{1,0:T(8,128)(2,1)S(1)}, bf16[512,768]{1,0:T(8,128)(2,1)}, u32[]{:S(2)}) copy-start(bf16[512,768]{1,0:T(8,128)(2,1)} %tgt_ref.1) | copy-start | bytes 2359300

commit v20 on v19

--- a/solution.py
+++ b/solution.py
@@ -43,12 +43,12 @@
     lax.fori_loop(0, count // 16, spread, 0)
 
 
-def mlp_block(dims, layer, w_in, w_out, hidden_ref, normed_ref, active_ref):
+def mlp_block(dims, layer, w_in, w_out, source_ref, hidden_ref, normed_ref, active_ref):
     layers, model_dim, hidden_dim, rows, chunks = dims
 
     def block(idx, _):
         at = pl.ds(pl.multiple_of(idx * 256, 256), 256)
-        hidden = hidden_ref[at, :].astype(F32)
+        hidden = source_ref[at, :].astype(F32)
         scale = lax.rsqrt(jnp.mean(hidden * hidden, axis=-1, keepdims=True) + NORM_EPS)
         normed_ref[...] = (hidden * scale).astype(BF16)
         for col in range(0, hidden_dim, 384):
@@ -56,7 +56,7 @@
             active_ref[:, col:col + 384] = jax.nn.gelu(inner.astype(F32), approximate=True).astype(BF16)
         for col in range(0, model_dim, 256):
             add = jnp.dot(active_ref[...], w_out[layer, :, col:col + 256], preferred_element_type=F32)
-            hidden_ref[at, col:col + 256] = (hidden_ref[at, col:col + 256].astype(F32) + add).astype(BF16)
+            hidden_ref[at, col:col + 256] = (source_ref[at, col:col + 256].astype(F32) + add).astype(BF16)
         return 0
 
     lax.fori_loop(0, rows // 256, block, 0)
@@ -142,13 +142,15 @@
         for which in range(1, 4):
             load(which, item).start()
     tok_load.start()
+    for which in range(1, 4):
+        load(which, 0).wait()
     for step in range(1, GROUP):
         part_arrival(step).wait_recv()
     total = part_ref[0]
     for slot in range(1, GROUP):
         total = total + part_ref[slot]
     total = jnp.sum(total, axis=1, keepdims=True)
-    clip = jnp.minimum(1.0, CLIP_NORM / jnp.sqrt(total))
+    clip = jnp.minimum(1.0, CLIP_NORM * lax.rsqrt(total))
     clip = jnp.broadcast_to(clip, (8, LANES))
 
     slots = {}
@@ -250,7 +252,7 @@
         lax.fori_loop(0, count // step // part[1], body, 0)
 
     for layer in range(layers):
-        for which in range(1, 4):
+        for which in range(1, 4) if layer else ():
             load(which, layer).wait()
         for part in own_parts(layer):
             adam(layer, part)
@@ -401,9 +403,9 @@
 
     by_kind(stage_own)
     tok_load.wait()
-    mlp_block(dims, 0, w_in, w_out, hidden_ref, normed_ref, active_ref)
+    mlp_block(dims, 0, w_in, w_out, hidden_ref, hidden_ref, normed_ref, active_ref)
     by_kind(stage_one)
-    mlp_block(dims, 1, w_in, w_out, hidden_ref, normed_ref, active_ref)
+    mlp_block(dims, 1, w_in, w_out, hidden_ref, hidden_ref, normed_ref, active_ref)
     by_kind(stage_two)
 
 
@@ -439,8 +441,7 @@
         far_copies.append(pltpu.make_async_copy(far_ref.at[idx], packed_hbm.at[pl.ds(device * chunks, chunks)], far_sem.at[idx]))
         far_copies[-1].start()
 
-    hidden_ref[...] = last_ref[...]
-    mlp_block(dims, layers - 1, w_in, w_out, hidden_ref, normed_ref, active_ref)
+    mlp_block(dims, layers - 1, w_in, w_out, last_ref, hidden_ref, normed_ref, active_ref)
 
     for idx in range(rows // LANES):
         at = slice(idx * LANES, (idx + 1) * LANES)

time: 63.3 us -> 63.3 us (level)
  no operation moved by 1% of the time
where the time goes in v20:
time: 63.3 us; the launch traced here: 63.2 us
  Pallas kernels  62.5 us (99%)
  between operations  0.66 us (1%)
    pallas_call x1, Pallas kernels, local_step(): pl.pallas_call(functools.partial(gather_kernel, dims), name='gather_step'...  54.9 us
    pallas_call x1, Pallas kernels, local_step(): pl.pallas_call(functools.partial(finish_kernel, dims), name='finish', out...  7.62 us

profile of v20, /device:TPU:0, one launch (start us, length us, event | category | flops | bytes accessed | tf_op | source)
XLA Modules:
  0.0 63.2 jit_solution(3748604217238674896)
XLA Ops:
  0.6 0.0 copy-start
  0.6 54.9 %gather_step.1 = (bf16[6912,128]{1,0:T(8,128)(2,1)S(1)}, bf16[6912,128]{1,0:T(8,128)(2,1)S(1)}, bf16[6912,128]{1,0:T(8,128)(2,1)S(1)}, bf16[6912,128]{1,0:T(8,12...) custom-call(f32[1728,3,128]{2,1,0:T(4,128)} %bitcast.43, ...), custom_call_target="tpu_custom_call" | custom-call | tf_op jit(solution)/shard_map/gather_step/pallas_call | solution.py:485
  55.6 0.0 copy-done
  55.6 7.6 %finish.1 = (bf16[13824,3,128]{2,1,0:T(4,128)(2,1)}, f32[1728,3,128]{2,1,0:T(4,128)}, f32[1728,3,128]{2,1,0:T(4,128)}, f32[1728,3,128]{2,1,0:T(4,128)}, f32[4,128]{1,0:T(4,128)}) custom-call(bf16[1728,3,128]{2,1,0:T(4,128)(2,1)S(1)} %bitcast.37, bf16[1728,3,128]{2,1,0:T(4,128)(2,1)S(1)} %bitcast.38, bf16[1728,3,128]{2,1,0:T(4,128)(2,1)S(1)} %bitcast.39, ...), custom_call_target="tpu_custom_call" | custom-call | tf_op jit(solution)/shard_map/finish/pallas_call | solution.py:506
Async XLA Ops:
  0.6 54.9 %copy-start = (bf16[512,768]{1,0:T(8,128)(2,1)S(1)}, bf16[512,768]{1,0:T(8,128)(2,1)}, u32[]{:S(2)}) copy-start(bf16[512,768]{1,0:T(8,128)(2,1)} %tgt_ref.1) | copy-start | bytes 2359300

commit v21 on v20

--- a/solution.py
+++ b/solution.py
@@ -90,14 +90,15 @@
         src, dst = state[which]
         return pltpu.make_async_copy(src.at[:, layer, :], dst.at[layer], load_sem.at[which, layer])
 
-    span = chunks // 3
+    loads = 1
+    span = chunks // loads
 
     def grad_load(layer, part):
         at = pl.ds(part * span, span)
         return pltpu.make_async_copy(grad_hbm.at[at, layer, :], grad_v.at[layer, at], grad_sem.at[layer, part])
 
     for layer in range(layers):
-        for part in range(3):
+        for part in range(loads):
             grad_load(layer, part).start()
     tok_load = pltpu.make_async_copy(tok_hbm, hidden_ref, load_sem.at[4, 0])
 
@@ -107,9 +108,9 @@
 
     sums = tuple(jnp.zeros((8, LANES), F32) for _ in range(8))
     for layer in range(layers):
-        for part in range(3):
+        for part in range(loads):
             grad_load(layer, part).wait()
-            if layer == layers - 1 and part == 2:
+            if layer == layers - 1 and part == loads - 1:
                 for which in range(1, 4):
                     load(which, 0).start()
 
@@ -150,7 +151,7 @@
     for slot in range(1, GROUP):
         total = total + part_ref[slot]
     total = jnp.sum(total, axis=1, keepdims=True)
-    clip = jnp.minimum(1.0, CLIP_NORM * lax.rsqrt(total))
+    clip = jnp.minimum(1.0, CLIP_NORM / jnp.sqrt(total))
     clip = jnp.broadcast_to(clip, (8, LANES))
 
     slots = {}

time: 63.3 us -> 63.5 us (level)
  no operation moved by 1% of the time
where the time goes in v21:
time: 63.5 us; the launch traced here: 63.4 us
  Pallas kernels  62.7 us (99%)
  between operations  0.66 us (1%)
    pallas_call x1, Pallas kernels, local_step(): pl.pallas_call(functools.partial(gather_kernel, dims), name='gather_step'...  55.1 us
    pallas_call x1, Pallas kernels, local_step(): pl.pallas_call(functools.partial(finish_kernel, dims), name='finish', out...  7.62 us

profile of v21, /device:TPU:0, one launch (start us, length us, event | category | flops | bytes accessed | tf_op | source)
XLA Modules:
  0.0 63.4 jit_solution(8908834095989864875)
XLA Ops:
  0.6 0.0 copy-start
  0.6 55.1 %gather_step.1 = (bf16[6912,128]{1,0:T(8,128)(2,1)S(1)}, bf16[6912,128]{1,0:T(8,128)(2,1)S(1)}, bf16[6912,128]{1,0:T(8,128)(2,1)S(1)}, bf16[6912,128]{1,0:T(8,12...) custom-call(f32[1728,3,128]{2,1,0:T(4,128)} %bitcast.43, ...), custom_call_target="tpu_custom_call" | custom-call | tf_op jit(solution)/shard_map/gather_step/pallas_call | solution.py:486
  55.7 0.0 copy-done
  55.7 7.6 %finish.1 = (bf16[13824,3,128]{2,1,0:T(4,128)(2,1)}, f32[1728,3,128]{2,1,0:T(4,128)}, f32[1728,3,128]{2,1,0:T(4,128)}, f32[1728,3,128]{2,1,0:T(4,128)}, f32[4,128]{1,0:T(4,128)}) custom-call(bf16[1728,3,128]{2,1,0:T(4,128)(2,1)S(1)} %bitcast.37, bf16[1728,3,128]{2,1,0:T(4,128)(2,1)S(1)} %bitcast.38, bf16[1728,3,128]{2,1,0:T(4,128)(2,1)S(1)} %bitcast.39, ...), custom_call_target="tpu_custom_call" | custom-call | tf_op jit(solution)/shard_map/finish/pallas_call | solution.py:507
Async XLA Ops:
  0.6 55.1 %copy-start = (bf16[512,768]{1,0:T(8,128)(2,1)S(1)}, bf16[512,768]{1,0:T(8,128)(2,1)}, u32[]{:S(2)}) copy-start(bf16[512,768]{1,0:T(8,128)(2,1)} %tgt_ref.1) | copy-start | bytes 2359300

commit v22 on v20

--- a/solution.py
+++ b/solution.py
@@ -150,7 +150,7 @@
     for slot in range(1, GROUP):
         total = total + part_ref[slot]
     total = jnp.sum(total, axis=1, keepdims=True)
-    clip = jnp.minimum(1.0, CLIP_NORM * lax.rsqrt(total))
+    clip = jnp.minimum(1.0, CLIP_NORM / jnp.sqrt(total))
     clip = jnp.broadcast_to(clip, (8, LANES))
 
     slots = {}
@@ -212,10 +212,11 @@
 
     def adam(layer, part):
         first = part[0] * (chunks // part[1])
+        step = 144 if part[1] == 12 else 48
 
         def update(idx, _):
-            base = pl.multiple_of(first + idx * 48, 8)
-            for k in range(6):
+            base = pl.multiple_of(first + idx * step, 8)
+            for k in range(step // 8):
                 at = pl.ds(pl.multiple_of(base + 8 * k, 8), 8)
                 clipped = grad_v[layer, at, :] * clip
                 new_one = BETA_ONE * one_v[layer, at, :] + (1.0 - BETA_ONE) * clipped
@@ -227,7 +228,7 @@
                 two_out[layer, at, :] = new_two
             return 0
 
-        lax.fori_loop(0, chunks // part[1] // 48, update, 0)
+        lax.fori_loop(0, chunks // part[1] // step, update, 0)
 
     def round_rows(kind, layer, part):
         width = hidden_dim if kind == 0 else model_dim

time: 63.3 us -> 63.3 us (level)
  no operation moved by 1% of the time
where the time goes in v22:
time: 63.3 us; the launch traced here: 63.2 us
  Pallas kernels  62.5 us (99%)
  between operations  0.66 us (1%)
    pallas_call x1, Pallas kernels, local_step(): pl.pallas_call(functools.partial(gather_kernel, dims), name='gather_step'...  54.9 us
    pallas_call x1, Pallas kernels, local_step(): pl.pallas_call(functools.partial(finish_kernel, dims), name='finish', out...  7.62 us

profile of v22, /device:TPU:0, one launch (start us, length us, event | category | flops | bytes accessed | tf_op | source)
XLA Modules:
  0.0 63.2 jit_solution(16674316487672028582)
XLA Ops:
  0.6 0.0 copy-start
  0.6 54.9 %gather_step.1 = (bf16[6912,128]{1,0:T(8,128)(2,1)S(1)}, bf16[6912,128]{1,0:T(8,128)(2,1)S(1)}, bf16[6912,128]{1,0:T(8,128)(2,1)S(1)}, bf16[6912,128]{1,0:T(8,12...) custom-call(f32[1728,3,128]{2,1,0:T(4,128)} %bitcast.43, ...), custom_call_target="tpu_custom_call" | custom-call | tf_op jit(solution)/shard_map/gather_step/pallas_call | solution.py:486
  55.5 0.0 copy-done
  55.6 7.6 %finish.1 = (bf16[13824,3,128]{2,1,0:T(4,128)(2,1)}, f32[1728,3,128]{2,1,0:T(4,128)}, f32[1728,3,128]{2,1,0:T(4,128)}, f32[1728,3,128]{2,1,0:T(4,128)}, f32[4,128]{1,0:T(4,128)}) custom-call(bf16[1728,3,128]{2,1,0:T(4,128)(2,1)S(1)} %bitcast.37, bf16[1728,3,128]{2,1,0:T(4,128)(2,1)S(1)} %bitcast.38, bf16[1728,3,128]{2,1,0:T(4,128)(2,1)S(1)} %bitcast.39, ...), custom_call_target="tpu_custom_call" | custom-call | tf_op jit(solution)/shard_map/finish/pallas_call | solution.py:507
Async XLA Ops:
  0.6 54.9 %copy-start = (bf16[512,768]{1,0:T(8,128)(2,1)S(1)}, bf16[512,768]{1,0:T(8,128)(2,1)}, u32[]{:S(2)}) copy-start(bf16[512,768]{1,0:T(8,128)(2,1)} %tgt_ref.1) | copy-start | bytes 2359300

commit v23 on v22

--- a/solution.py
+++ b/solution.py
@@ -138,10 +138,6 @@
 
     for step in range(1, GROUP):
         part_copy(step).start()
-    for item in range(1, layers):
-        for which in range(1, 4):
-            load(which, item).start()
-    tok_load.start()
     for which in range(1, 4):
         load(which, 0).wait()
     for step in range(1, GROUP):
@@ -266,6 +262,11 @@
                 start(pair(kind, layer, me, "pair_own", (part,)))
 
             by_kind(send_own)
+            if layer == 0 and part == own_parts(0)[0]:
+                for item in range(1, layers):
+                    for which in range(1, 4):
+                        load(which, item).start()
+                tok_load.start()
 
     def pack(kind, device, packed_ref):
         spread_piece(dims, kind, device, (w_in, w_out), wide_ref)

time: 63.3 us -> 63.3 us (level)
  no operation moved by 1% of the time
where the time goes in v23:
time: 63.3 us; the launch traced here: 63.2 us
  Pallas kernels  62.5 us (99%)
  between operations  0.66 us (1%)
    pallas_call x1, Pallas kernels, local_step(): pl.pallas_call(functools.partial(gather_kernel, dims), name='gather_step'...  54.9 us
    pallas_call x1, Pallas kernels, local_step(): pl.pallas_call(functools.partial(finish_kernel, dims), name='finish', out...  7.62 us

profile of v23, /device:TPU:0, one launch (start us, length us, event | category | flops | bytes accessed | tf_op | source)
XLA Modules:
  0.0 63.2 jit_solution(9939707552149423175)
XLA Ops:
  0.6 0.0 copy-start
  0.6 54.9 %gather_step.1 = (bf16[6912,128]{1,0:T(8,128)(2,1)S(1)}, bf16[6912,128]{1,0:T(8,128)(2,1)S(1)}, bf16[6912,128]{1,0:T(8,128)(2,1)S(1)}, bf16[6912,128]{1,0:T(8,12...) custom-call(f32[1728,3,128]{2,1,0:T(4,128)} %bitcast.43, ...), custom_call_target="tpu_custom_call" | custom-call | tf_op jit(solution)/shard_map/gather_step/pallas_call | solution.py:487
  55.5 0.0 copy-done
  55.6 7.6 %finish.1 = (bf16[13824,3,128]{2,1,0:T(4,128)(2,1)}, f32[1728,3,128]{2,1,0:T(4,128)}, f32[1728,3,128]{2,1,0:T(4,128)}, f32[1728,3,128]{2,1,0:T(4,128)}, f32[4,128]{1,0:T(4,128)}) custom-call(bf16[1728,3,128]{2,1,0:T(4,128)(2,1)S(1)} %bitcast.37, bf16[1728,3,128]{2,1,0:T(4,128)(2,1)S(1)} %bitcast.38, bf16[1728,3,128]{2,1,0:T(4,128)(2,1)S(1)} %bitcast.39, ...), custom_call_target="tpu_custom_call" | custom-call | tf_op jit(solution)/shard_map/finish/pallas_call | solution.py:508
Async XLA Ops:
  0.6 54.9 %copy-start = (bf16[512,768]{1,0:T(8,128)(2,1)S(1)}, bf16[512,768]{1,0:T(8,128)(2,1)}, u32[]{:S(2)}) copy-start(bf16[512,768]{1,0:T(8,128)(2,1)} %tgt_ref.1) | copy-start | bytes 2359300

commit v24 on v22

--- a/solution.py
+++ b/solution.py
@@ -423,8 +423,8 @@
             copies.append(pltpu.make_async_copy(src.at[layer], dst.at[:, layer, :], sem.at[6 + which * layers + layer]))
     for idx, (ref, device) in enumerate(((p0, me), (p1, me + twin), (p2, x_peer), (p3, x_peer + twin), (p4, y_peer), (p5, y_peer + twin))):
         copies.append(pltpu.make_async_copy(ref, packed_hbm.at[pl.ds(device * chunks, chunks)], sem.at[idx]))
-    for item in copies:
-        item.start()
+    for idx, item in enumerate(copies):
+        item.start(priority=idx % 2)
 
     far_copies = []
     for idx, device in enumerate((diag, diag + twin)):

time: 63.3 us -> 63.3 us (level)
  no operation moved by 1% of the time
where the time goes in v24:
time: 63.3 us; the launch traced here: 63.2 us
  Pallas kernels  62.5 us (99%)
  between operations  0.66 us (1%)
    pallas_call x1, Pallas kernels, local_step(): pl.pallas_call(functools.partial(gather_kernel, dims), name='gather_step'...  54.9 us
    pallas_call x1, Pallas kernels, local_step(): pl.pallas_call(functools.partial(finish_kernel, dims), name='finish', out...  7.62 us

profile of v24, /device:TPU:0, one launch (start us, length us, event | category | flops | bytes accessed | tf_op | source)
XLA Modules:
  0.0 63.2 jit_solution(18405217357551268369)
XLA Ops:
  0.6 0.0 copy-start
  0.6 54.9 %gather_step.1 = (bf16[6912,128]{1,0:T(8,128)(2,1)S(1)}, bf16[6912,128]{1,0:T(8,128)(2,1)S(1)}, bf16[6912,128]{1,0:T(8,128)(2,1)S(1)}, bf16[6912,128]{1,0:T(8,12...) custom-call(f32[1728,3,128]{2,1,0:T(4,128)} %bitcast.43, ...), custom_call_target="tpu_custom_call" | custom-call | tf_op jit(solution)/shard_map/gather_step/pallas_call | solution.py:486
  55.5 0.0 copy-done
  55.6 7.6 %finish.1 = (bf16[13824,3,128]{2,1,0:T(4,128)(2,1)}, f32[1728,3,128]{2,1,0:T(4,128)}, f32[1728,3,128]{2,1,0:T(4,128)}, f32[1728,3,128]{2,1,0:T(4,128)}, f32[4,128]{1,0:T(4,128)}) custom-call(bf16[1728,3,128]{2,1,0:T(4,128)(2,1)S(1)} %bitcast.37, bf16[1728,3,128]{2,1,0:T(4,128)(2,1)S(1)} %bitcast.38, bf16[1728,3,128]{2,1,0:T(4,128)(2,1)S(1)} %bitcast.39, ...), custom_call_target="tpu_custom_call" | custom-call | tf_op jit(solution)/shard_map/finish/pallas_call | solution.py:507
Async XLA Ops:
  0.6 54.9 %copy-start = (bf16[512,768]{1,0:T(8,128)(2,1)S(1)}, bf16[512,768]{1,0:T(8,128)(2,1)}, u32[]{:S(2)}) copy-start(bf16[512,768]{1,0:T(8,128)(2,1)} %tgt_ref.1) | copy-start | bytes 2359300
